TPU v7x, 8 devices: a whole 2x2x1 slice. The times are simulated.
8 devices in a mesh: bs: 2 (over z, y), tp: 4 (over x, core).
Axes of the slice: x: 2, y: 2, z: 1, core: 2. Of those that a mesh axis runs over, the one named last changes fastest.
Arguments:
- new_hidden: bfloat16 [512, 2560], P('bs'), parts along dimension 0
- cache_k: bfloat16 [512, 64, 32, 80], P('bs', None, 'tp'), parts along dimension 0
- cache_v: bfloat16 [512, 64, 32, 80], P('bs', None, 'tp'), parts along dimension 0
- lengths: int32 [512], P('bs'), parts along dimension 0
- ln1_gain: float32 [2560], replicated
- ln1_bias: float32 [2560], replicated
- w_q: bfloat16 [2560, 2560], P(None, 'tp')
- w_k: bfloat16 [2560, 2560], P(None, 'tp')
- w_v: bfloat16 [2560, 2560], P(None, 'tp')
- w_o: bfloat16 [2560, 2560], P('tp')
- ln2_gain: float32 [2560], replicated
- ln2_bias: float32 [2560], replicated
- w_up: bfloat16 [2560, 10240], P(None, 'tp')
- w_down: bfloat16 [10240, 2560], P('tp')
- lnf_gain: float32 [2560], replicated
- lnf_bias: float32 [2560], replicated
- w_out: bfloat16 [2560, 51200], P(None, 'tp')
Outputs:
- output 1: float32 [512, 51200], P('bs', 'tp'), parts along dimension 0
- output 2: bfloat16 [512, 64, 32, 80], P('bs', None, 'tp'), parts along dimension 0
- output 3: bfloat16 [512, 64, 32, 80], P('bs', None, 'tp'), parts along dimension 0
- output 4: bfloat16 [512, 2560], P('bs'), parts along dimension 0
There are 2 independent parts. A program takes and returns all parts, laid end to end along the dimension named above; an argument that names none is the same for every part.
All inputs are finite; a program needn't handle non-finite values.
Results may differ from a plain program's by a relative error of at most 0.0149567.
Values are sent between devices in bfloat16 or wider.
A program may use at most 1 GiB of HBM per device.

v0:
```python
import jax
import jax.numpy as jnp
from jax import lax
from jax.sharding import PartitionSpec as P

EPSILON = 1e-5
ROPE_BASE = 10000.0


def layer_norm1p(values, gain, bias):
    mean = jnp.mean(values, axis=-1, keepdims=True)
    centered = values - mean
    variance = jnp.mean(jnp.square(centered), axis=-1, keepdims=True)
    return centered * lax.rsqrt(variance + EPSILON) * (1.0 + gain) + bias


def apply_rotary(vecs, positions):
    rot_dim = vecs.shape[-1] // 2
    half_rot = rot_dim // 2
    exponent = -2.0 * jnp.arange(half_rot, dtype=jnp.float32) / rot_dim
    inv_freq = ROPE_BASE ** exponent
    angles = positions.astype(jnp.float32)[:, None] * inv_freq[None, :]
    cosine = jnp.cos(angles)[:, None, :]
    sine = jnp.sin(angles)[:, None, :]
    first = vecs[..., :half_rot]
    second = vecs[..., half_rot:rot_dim]
    return jnp.concatenate([first * cosine - second * sine, second * cosine + first * sine, vecs[..., rot_dim:]], axis=-1)


def project_and_attend(new_hidden, cache_k, cache_v, lengths, ln1_gain, ln1_bias, w_q, w_k, w_v):
    batch, cache_len, kv_heads, head_dim = cache_k.shape
    normed = layer_norm1p(new_hidden.astype(jnp.float32), ln1_gain, ln1_bias).astype(jnp.bfloat16)
    query = jnp.dot(normed, w_q, preferred_element_type=jnp.float32).reshape(batch, -1, head_dim)
    key_new = jnp.dot(normed, w_k, preferred_element_type=jnp.float32).reshape(batch, kv_heads, head_dim)
    val_new = jnp.dot(normed, w_v, preferred_element_type=jnp.float32).reshape(batch, kv_heads, head_dim)
    query = apply_rotary(query, lengths).astype(jnp.bfloat16)
    key_new = apply_rotary(key_new, lengths).astype(jnp.bfloat16)
    val_new = val_new.astype(jnp.bfloat16)
    positions = jnp.arange(cache_len)
    write_slot = (positions[None, :] == lengths[:, None])[:, :, None, None]
    new_cache_k = jnp.where(write_slot, key_new[:, None], cache_k)
    new_cache_v = jnp.where(write_slot, val_new[:, None], cache_v)
    group = query.shape[1] // kv_heads
    q_groups = query.reshape(batch, kv_heads, group, head_dim)
    score_scale = head_dim ** -0.5
    scores = jnp.einsum('bgrk,blgk->bgrl', q_groups, new_cache_k, preferred_element_type=jnp.float32) * score_scale
    valid = (positions[None, :] <= lengths[:, None])[:, None, None, :]
    scores = jnp.where(valid, scores, -1e30)
    attn_prob = jax.nn.softmax(scores, axis=-1).astype(jnp.bfloat16)
    mixed = jnp.einsum('bgrl,blgk->bgrk', attn_prob, new_cache_v, preferred_element_type=jnp.float32)
    return mixed.astype(jnp.bfloat16).reshape(batch, -1), new_cache_k, new_cache_v


def reduce_to_all(partial, residual, ways):
    batch, width = partial.shape
    piece = width // ways
    received = lax.all_to_all(partial, 'tp', 1, 0, tiled=True)
    summed = jnp.sum(received.reshape(ways, batch, piece).astype(jnp.float32), axis=0)
    start = lax.axis_index('tp') * piece
    own_resid = lax.dynamic_slice_in_dim(residual, start, piece, axis=1)
    own_sum = (own_resid.astype(jnp.float32) + summed).astype(jnp.bfloat16)
    return lax.all_gather(own_sum, 'tp', axis=1, tiled=True)


def solution(mesh):
    ways = mesh.shape['tp']
    row_spec = P('bs', None)
    cache_spec = P('bs', None, 'tp', None)
    col_split = P(None, 'tp')
    row_split = P('tp', None)
    in_specs = (row_spec, cache_spec, cache_spec, P('bs'), P(), P(), col_split, col_split, col_split, row_split, P(), P(), col_split, row_split, P(), P(), col_split)
    out_specs = (P('bs', 'tp'), cache_spec, cache_spec, row_spec)

    def local_step(new_hidden, cache_k, cache_v, lengths, ln1_gain, ln1_bias, w_q, w_k, w_v, w_o, ln2_gain, ln2_bias, w_up, w_down, lnf_gain, lnf_bias, w_out):
        attended, new_cache_k, new_cache_v = project_and_attend(new_hidden, cache_k, cache_v, lengths, ln1_gain, ln1_bias, w_q, w_k, w_v)
        partial_o = jnp.dot(attended, w_o, preferred_element_type=jnp.float32).astype(jnp.bfloat16)
        mid_hidden = reduce_to_all(partial_o, new_hidden, ways)
        normed_mid = layer_norm1p(mid_hidden.astype(jnp.float32), ln2_gain, ln2_bias).astype(jnp.bfloat16)
        up_proj = jnp.dot(normed_mid, w_up, preferred_element_type=jnp.float32)
        activated = jnp.square(jnp.maximum(up_proj, 0.0)).astype(jnp.bfloat16)
        partial_m = jnp.dot(activated, w_down, preferred_element_type=jnp.float32).astype(jnp.bfloat16)
        out_hidden = reduce_to_all(partial_m, mid_hidden, ways)
        normed_out = layer_norm1p(out_hidden.astype(jnp.float32), lnf_gain, lnf_bias).astype(jnp.bfloat16)
        logits = jnp.dot(normed_out, w_out, preferred_element_type=jnp.float32)
        local_peak = jnp.max(logits, axis=-1)
        local_total = jnp.sum(jnp.exp(logits - local_peak[:, None]), axis=-1)
        gathered = lax.all_gather(jnp.stack([local_peak, local_total]), 'tp')
        global_peak = jnp.max(gathered[:, 0], axis=0)
        global_total = jnp.sum(gathered[:, 1] * jnp.exp(gathered[:, 0] - global_peak[None, :]), axis=0)
        log_probs = logits - (global_peak + jnp.log(global_total))[:, None]
        return log_probs, new_cache_k, new_cache_v, out_hidden

    return jax.shard_map(local_step, mesh=mesh, in_specs=in_specs, out_specs=out_specs, check_vma=False)
```

profile of v0, /device:TPU:0, one launch (start us, length us, event | category | flops | bytes accessed | tf_op | source)
XLA Modules:
  0.0 241.7 jit_solution(9283668300827415188)
XLA Ops:
  10.5 1.8 fusion.18
  12.3 3.9 %convolution_convert_fusion.2 = bf16[256,640]{1,0:T(8,128)(2,1)} fusion(bf16[2560,640]{1,0:T(8,128)(2,1)} %param.25, bf16[256,2560]{1,0:T(8,128)(2,1)S(1)} %copy-done.3, f32[2560]{0:T(1024)S(1)} %copy-done.10, f32[2560]{0:T(1024)S(1)} %broadcast_add_fusion.2, f32[256]{0:T(256)S(1)} %add_rsqrt_fusion.2, f32[256]{0:T(256)S(1)} %broadcast_multiply_fusion.2), kind=kOutput, calls=%fused_computation.53 | convolution fusion | flops 842956800 | bytes 4937728 | tf_op jit(solution)/shard_map/dot_general | solution.py:35
  16.3 1.9 copy.39
  18.1 4.1 %fusion.60 = f32[256,640]{0,1:T(8,128)S(1)} fusion(bf16[2560,640]{1,0:T(8,128)(2,1)} %param.24, bf16[256,2560]{1,0:T(8,128)(2,1)} %param.17, f32[2560]{0:T(1024)S(1)} %copy-done.10, f32[2560]{0:T(1024)S(1)} %broadcast_add_fusion.2, f32[256]{0:T(256)S(1)} %add_rsqrt_fusion.2, f32[256]{0:T(256)S(1)} %broadcast_multiply_fusion.2), kind=kOutput, calls=%fused_computation.100 | convolution fusion | flops 842792960 | bytes 5265408 | tf_op jit(solution)/shard_map/dot_general | solution.py:34
  22.3 1.7 fusion.62
  24.4 23.6 %multiply_reduce_fusion.1 = (f32[256,8,64]{0,1,2:T(8,128)}, bf16[256,64,8,80]{0,3,2,1:T(8,128)(2,1)}) fusion(f32[256,8,80]{0,2,1:T(8,128)S(1)} %get-tuple-element.23, bf16[256,64,8,80]{0,3,2,1:T(8,128)(2,1)} %param.18, bf16[256,8,80]{0,2,1:T(8,128)(2,1)S(1)} %get-tuple-element.24, pred[256,64]{0,1:T(8,128)(4,1)S(1)} %get-tuple-element.20), kind=kLoop, calls=%fused_computation.3 | loop fusion | flops 41811968 | bytes 43466752
  48.1 2.2 fusion.37
  51.6 21.6 %multiply_reduce_fusion = (bf16[256,8,80]{0,2,1:T(8,128)(2,1)S(1)}, bf16[256,64,8,80]{0,3,2,1:T(8,128)(2,1)}) fusion(f32[256,8,64]{0,1,2:T(8,128)S(1)} %copy.61, bf16[256,64,8,80]{0,3,2,1:T(8,128)(2,1)} %param.19, bf16[256,8,80]{0,2,1:T(8,128)(2,1)} %bitcast.41, pred[256,64]{0,1:T(8,128)(4,1)S(1)} %get-tuple-element.20), kind=kLoop, calls=%fused_computation.2 | loop fusion | flops 41779200 | bytes 43139072 | tf_op jit(solution)/shard_map/bgrl,blgk->bgrk/dot_general | solution.py:50
  75.6 4.8 %all-to-all-start = ((bf16[256,4,640]{2,0,1:T(8,128)(2,1)}), bf16[256,4,640]{2,0,1:T(8,128)(2,1)S(1)}, u32[]{:S(2)}, u32[]{:S(2)}) async-start(bf16[256,4,640]{2,0,1:T(8,128)(2,1)} %bitcast.39), calls=%async_computation | async-start | bytes 2621440 | tf_op jit(solution)/shard_map/all_to_all | solution.py:57
  80.3 17.0 %all-to-all-done = bf16[256,4,640]{2,0,1:T(8,128)(2,1)S(1)} async-done(((bf16[256,4,640]{2,0,1:T(8,128)(2,1)}), bf16[256,4,640]{2,0,1:T(8,128)(2,1)S(1)}, u32[]{:S(2)}, u32[]{:S(2)}) %all-to-all-start) | async-done | bytes 1310752 | tf_op jit(solution)/shard_map/all_to_all | solution.py:57
  97.5 1.8 add_convert_fusion.1
  99.6 15.9 %all-gather.5.cloned.1.call-done = bf16[256,2560]{1,0:T(8,128)(2,1)} async-done(((bf16[256,640]{1,0:T(8,128)(2,1)}), bf16[256,2560]{1,0:T(8,128)(2,1)}) %all-gather.5.cloned.1.call-update) | async-done | bytes 1310736 | tf_op jit(solution)/shard_map/all_gather | solution.py:62
  115.4 1.7 convert_reduce_fusion.1
  117.1 1.8 fusion.14
  119.0 16.5 %convolution_convert_fusion.1 = bf16[256,2560]{1,0:T(8,128)(2,1)} fusion(bf16[2560,2560]{1,0:T(8,128)(2,1)} %param.30, bf16[2560,2560]{1,0:T(8,128)(2,1)} %param.29, bf16[256,2560]{1,0:T(8,128)(2,1)S(1)} %copy-done.5, f32[2560]{0:T(1024)S(1)} %copy-done.11, f32[2560]{0:T(1024)S(1)} %broadcast_add_fusion.1, f32[256]{0:T(256)S(1)} %add_rsqrt_fusion.1, ...), kind=kOutput, calls=%fused_computation.12 | convolution fusion | flops 6717440000 | bytes 28858368 | tf_op jit(solution)/shard_map/dot_general | solution.py:81
  136.9 19.7 %all_to_all.26 = bf16[256,4,640]{2,0,1:T(8,128)(2,1)S(1)} all-to-all(bf16[256,4,640]{2,0,1:T(8,128)(2,1)S(1)} %bitcast.40), channel_id=1, replica_groups=mesh['bs'=2,'tp'=4] {'tp'}, dimensions={1} | all-to-all | bytes 2621440 | tf_op jit(solution)/shard_map/all_to_all | solution.py:57
  157.6 15.3 %all-gather.7.cloned.1.call-done = bf16[256,2560]{1,0:T(8,128)(2,1)} async-done(((bf16[256,640]{1,0:T(8,128)(2,1)}), bf16[256,2560]{1,0:T(8,128)(2,1)}) %all-gather.7.cloned.1.call-update) | async-done | bytes 1310736 | tf_op jit(solution)/shard_map/all_gather | solution.py:62
  172.9 1.7 convert_reduce_fusion
  174.6 1.8 fusion.10
  176.4 31.4 %fusion.65 = (f32[256]{0:T(256)S(1)}, f32[256,12800]{1,0:T(8,128)}) fusion(bf16[2560,12800]{1,0:T(8,128)(2,1)} %param.33, bf16[256,2560]{1,0:T(8,128)(2,1)S(1)} %copy-done.2, f32[2560]{0:T(1024)S(1)} %copy-done.12, f32[2560]{0:T(1024)S(1)} %broadcast_add_fusion, f32[256]{0:T(256)S(1)} %add_rsqrt_fusion, f32[256]{0:T(256)S(1)} %broadcast_multiply_fusion), kind=kOutput, calls=%fused_computation.103 | convolution fusion | flops 16784424960 | bytes 79977472 | tf_op jit(solution)/shard_map/dot_general | solution.py:84
  207.8 6.6 %exponential_reduce_fusion = f32[256]{0:T(256)S(1)} fusion(f32[256,12800]{1,0:T(8,128)} %get-tuple-element.22, f32[256]{0:T(256)S(1)} %get-tuple-element.21), kind=kLoop, calls=%fused_computation.6 | loop fusion | flops 6553344 | bytes 13109248 | tf_op jit(solution)/shard_map/reduce_sum | solution.py:86
  214.4 6.8 %all-gather.1 = f32[4,2,256]{2,1,0:T(2,128)S(1)} all-gather(f32[1,2,256]{2,1,0:T(2,128)S(1)} %maximum_bitcast_fusion), channel_id=2, replica_groups=mesh['bs'=2,'tp'=4] {'tp'}, dimensions={0}, use_global_device_ids=true | all-gather | bytes 10240 | tf_op jit(solution)/shard_map/all_gather | solution.py:87
  221.3 11.1 %broadcast_subtract_fusion = f32[256,12800]{1,0:T(8,128)} fusion(f32[256,12800]{1,0:T(8,128)} %get-tuple-element.22, f32[256]{0:T(256)S(1)} %log_add_fusion), kind=kLoop, calls=%fused_computation.7 | loop fusion | flops 3276800 | bytes 26215424 | tf_op jit(solution)/shard_map/sub | solution.py:90
  232.4 2.5 %copy.84 = bf16[256,2560]{1,0:T(8,128)(2,1)} copy(bf16[256,2560]{1,0:T(8,128)(2,1)} %all-gather.7.cloned.1.call-done) | data formatting | bytes 2621440
  (59 shorter events, 10.5 us)
Async XLA Ops:
  7.2 66.0 %copy-start = (bf16[640,2560]{1,0:T(8,128)(2,1)S(1)}, bf16[640,2560]{1,0:T(8,128)(2,1)}, u32[]{:S(2)}) copy-start(bf16[640,2560]{1,0:T(8,128)(2,1)} %param.26) | copy-start | bytes 9830404
  7.2 5.1 %copy-start.3 = (bf16[256,2560]{1,0:T(8,128)(2,1)S(1)}, bf16[256,2560]{1,0:T(8,128)(2,1)}, u32[]{:S(2)}) copy-start(bf16[256,2560]{1,0:T(8,128)(2,1)} %param.17) | copy-start | bytes 3932164
  7.2 5.1 %copy-start.6 = (f32[2560]{0:T(1024)S(1)}, f32[2560]{0:T(1024)}, u32[]{:S(2)}) copy-start(f32[2560]{0:T(1024)} %param.21) | copy-start | bytes 30724
  7.2 5.1 %copy-start.10 = (f32[2560]{0:T(1024)S(1)}, f32[2560]{0:T(1024)}, u32[]{:S(2)}) copy-start(f32[2560]{0:T(1024)} %param.22) | copy-start | bytes 30724
  18.1 4.1 %copy-start.4 = (bf16[256,2560]{1,0:T(8,128)(2,1)S(1)}, bf16[256,2560]{1,0:T(8,128)(2,1)}, u32[]{:S(2)}) copy-start(bf16[256,2560]{1,0:T(8,128)(2,1)} %param.17) | copy-start | bytes 3932164
  18.1 4.1 %copy-start.9 = (bf16[2560,640]{1,0:T(8,128)(2,1)S(1)}, bf16[2560,640]{1,0:T(8,128)(2,1)}, u32[]{:S(2)}) copy-start(bf16[2560,640]{1,0:T(8,128)(2,1)} %param.23) | copy-start | bytes 9830404
  75.6 24.0 %copy-start.7 = (f32[2560]{0:T(1024)S(1)}, f32[2560]{0:T(1024)}, u32[]{:S(2)}) copy-start(f32[2560]{0:T(1024)} %param.27) | copy-start | bytes 30724
  75.6 21.8 %all-to-all-start = ((bf16[256,4,640]{2,0,1:T(8,128)(2,1)}), bf16[256,4,640]{2,0,1:T(8,128)(2,1)S(1)}, u32[]{:S(2)}, u32[]{:S(2)}) async-start(bf16[256,4,640]{2,0,1:T(8,128)(2,1)} %bitcast.39), calls=%async_computation | async-start | bytes 2621440 | tf_op jit(solution)/shard_map/all_to_all | solution.py:57
  80.3 35.1 %all-gather.5.cloned.1.call-start = ((), (), s32[]{:S(2)}) async-start(), calls=%async_computation.2 | async-start | bytes 1638400 | tf_op jit(solution)/shard_map/all_gather | solution.py:62
  97.5 21.4 %copy-start.11 = (f32[2560]{0:T(1024)S(1)}, f32[2560]{0:T(1024)}, u32[]{:S(2)}) copy-start(f32[2560]{0:T(1024)} %param.28) | copy-start | bytes 30724
  99.3 73.6 %all-gather.7.cloned.1.call-start = ((), (), s32[]{:S(2)}) async-start(), calls=%async_computation.3 | async-start | bytes 1638400 | tf_op jit(solution)/shard_map/all_gather | solution.py:62
  115.4 3.5 %copy-start.5 = (bf16[256,2560]{1,0:T(8,128)(2,1)S(1)}, bf16[256,2560]{1,0:T(8,128)(2,1)}, u32[]{:S(2)}) copy-start(bf16[256,2560]{1,0:T(8,128)(2,1)} %all-gather.5.cloned.1.call-done) | copy-start | bytes 3932164
  136.9 20.7 %copy-start.8 = (f32[2560]{0:T(1024)S(1)}, f32[2560]{0:T(1024)}, u32[]{:S(2)}) copy-start(f32[2560]{0:T(1024)} %param.31) | copy-start | bytes 30724
  156.8 19.6 %copy-start.12 = (f32[2560]{0:T(1024)S(1)}, f32[2560]{0:T(1024)}, u32[]{:S(2)}) copy-start(f32[2560]{0:T(1024)} %param.32) | copy-start | bytes 30724
  172.9 3.5 %copy-start.2 = (bf16[256,2560]{1,0:T(8,128)(2,1)S(1)}, bf16[256,2560]{1,0:T(8,128)(2,1)}, u32[]{:S(2)}) copy-start(bf16[256,2560]{1,0:T(8,128)(2,1)} %all-gather.7.cloned.1.call-done) | copy-start | bytes 3932164
  221.3 13.6 %copy-start.1 = (bf16[640,2560]{1,0:T(8,128)(2,1)S(1)}, bf16[640,2560]{1,0:T(8,128)(2,1)}, u32[]{:S(2)}) copy-start(bf16[640,2560]{1,0:T(8,128)(2,1)} %param.26) | copy-start | bytes 9830404
Sparse Core Ops, SparseCore 0:
  99.4 15.9 all-gather.4
  157.7 15.1 all-gather.6
where the time goes:
time: 243 us; the launch traced here: 242 us
  other arithmetic  80.5 us (33%)
  matrix products  58.8 us (24%)
  waiting for transfers between devices  48.2 us (20%)
  blocking collectives  26.5 us (11%)
  between operations  14.3 us (6%)
  local copies, waits for them, and re-layouts  8.37 us (3%)
  starting transfers between devices  4.98 us (2%)
    dot_general x1, matrix products, local_step(): logits = jnp.dot(normed_out, w_out, preferred_element_type=jnp.float32)  31.4 us
    all_gather x2, waiting for transfers between devices, reduce_to_all(): return lax.all_gather(own_sum, 'tp', axis=1, tiled=True)  31.2 us
    unnamed x3, other arithmetic  23.8 us
    dot_general x1, other arithmetic, project_and_attend(): jnp.einsum('bgrl,blgk->bgrk', attn_prob, new_cache_v, preferred_element_t...  21.6 us
    all_to_all x1, blocking collectives, reduce_to_all(): received = lax.all_to_all(partial, 'tp', 1, 0, tiled=True)  19.7 us
    all_to_all x1, waiting for transfers between devices, reduce_to_all(): received = lax.all_to_all(partial, 'tp', 1, 0, tiled=True)  17 us
    dot_general x1, matrix products, local_step(): jnp.dot(activated, w_down, preferred_element_type=jnp.float32)  16.5 us
    sub x1, other arithmetic, local_step(): log_probs = logits - (global_peak + jnp.log(global_total))[:, None]  11.1 us
  transfers between devices with their start and end apart: 3, of which 3 were waited for; matrix products, arithmetic and copies ran while one was open for 0% of the time, Pallas kernels for 0%

commit v1 on v0

v1 whole, which is shorter than its diff:
```python
import jax
import jax.numpy as jnp
import numpy as np
from jax import lax
from jax.experimental import pallas as pl
from jax.experimental.pallas import tpu as pltpu
from jax.sharding import PartitionSpec as P

EPSILON = 1e-5
ROPE_BASE = 10000.0
AHEAD = 2
VMEM_LIMIT = 66 * 1000 * 1000


def norm_block(values, gain, bias):
    mean = jnp.mean(values, axis=-1, keepdims=True)
    centered = values - mean
    variance = jnp.mean(jnp.square(centered), axis=-1, keepdims=True)
    return centered * lax.rsqrt(variance + EPSILON) * (1.0 + gain) + bias


def attention_kernel(x_ref, len_ref, freq_ref, gain_ref, bias_ref, wq_hbm, wk_hbm, wv_hbm, wo_hbm, kc_hbm, vc_hbm, part_ref, ko_hbm, vo_hbm, kbuf, vbuf, wbuf, wobuf, h_ref, qkv_ref, tmp_ref, attn_ref, s_ref, w_sem, ki_sem, vi_sem, ko_sem, vo_sem):
    heads, cache_len, head_dim, batch = kbuf.shape
    half_rot = head_dim // 4
    weight_copies = [pltpu.make_async_copy(src, wbuf.at[i], w_sem.at[i]) for i, src in enumerate((wq_hbm, wk_hbm, wv_hbm))]

    def k_in(h):
        return pltpu.make_async_copy(kc_hbm.at[:, h], kbuf.at[h], ki_sem.at[h])

    def v_in(h):
        return pltpu.make_async_copy(vc_hbm.at[:, h], vbuf.at[h], vi_sem.at[h])

    def k_out(h):
        return pltpu.make_async_copy(kbuf.at[h], ko_hbm.at[:, h], ko_sem.at[h])

    def v_out(h):
        return pltpu.make_async_copy(vbuf.at[h], vo_hbm.at[:, h], vo_sem.at[h])

    wo_copy = pltpu.make_async_copy(wo_hbm, wobuf, w_sem.at[3])
    for copy in weight_copies:
        copy.start()
    for h in range(AHEAD):
        k_in(h).start()
        v_in(h).start()

    rows = 32

    def norm_rows(i, carry):
        here = pl.ds(pl.multiple_of(i * rows, rows), rows)
        h_ref[here, :] = norm_block(x_ref[here, :].astype(jnp.float32), gain_ref[...], bias_ref[...]).astype(jnp.bfloat16)
        return carry

    lax.fori_loop(0, batch // rows, norm_rows, 0)

    angles = freq_ref[...] * len_ref[...].astype(jnp.float32)
    upper = lax.broadcasted_iota(jnp.int32, angles.shape, 0) < half_rot
    cosine = jnp.cos(angles)
    sine = jnp.where(upper, -jnp.sin(angles), jnp.sin(angles))

    for i in range(3):
        weight_copies[i].wait()
        flat = jnp.dot(h_ref[...], wbuf[i], preferred_element_type=jnp.float32)
        tmp_ref[...] = flat.T
        for h in range(heads):
            base = h * head_dim
            out = pl.ds(h * head_dim, head_dim)
            if i == 2:
                qkv_ref[i, out, :] = tmp_ref[out, :]
            else:
                first = tmp_ref[pl.ds(base, half_rot), :]
                second = tmp_ref[pl.ds(base + half_rot, half_rot), :]
                both = tmp_ref[pl.ds(base, 2 * half_rot), :]
                swapped = jnp.concatenate([second, first], axis=0)
                qkv_ref[i, pl.ds(base, 2 * half_rot), :] = both * cosine + swapped * sine
                rest = pl.ds(base + 2 * half_rot, head_dim - 2 * half_rot)
                qkv_ref[i, rest, :] = tmp_ref[rest, :]
    wo_copy.start()
    scale = head_dim ** -0.5
    lengths = len_ref[...]

    def one_head(h, carry):
        @pl.when(h + AHEAD < heads)
        def _():
            k_in(h + AHEAD).start()
            v_in(h + AHEAD).start()

        here = pl.ds(pl.multiple_of(h * head_dim, head_dim), head_dim)
        query = qkv_ref[0, here, :].astype(jnp.bfloat16).astype(jnp.float32)
        key_new = qkv_ref[1, here, :].astype(jnp.bfloat16)
        val_new = qkv_ref[2, here, :].astype(jnp.bfloat16)
        k_in(h).wait()

        def score_row(l, c):
            old = kbuf[h, l]
            row = jnp.where(jnp.broadcast_to(lengths == l, old.shape), key_new, old)
            kbuf[h, l] = row
            s_ref[pl.ds(l, 1), :] = jnp.sum(row.astype(jnp.float32) * query, axis=0, keepdims=True)
            return c

        lax.fori_loop(0, cache_len, score_row, 0, unroll=4)
        k_out(h).start()
        scores = s_ref[...] * scale
        valid = lax.broadcasted_iota(jnp.int32, scores.shape, 0) <= lengths
        scores = jnp.where(valid, scores, -1e30)
        weights = jnp.exp(scores - jnp.max(scores, axis=0, keepdims=True))
        s_ref[...] = (weights / jnp.sum(weights, axis=0, keepdims=True)).astype(jnp.bfloat16).astype(jnp.float32)
        v_in(h).wait()

        def mix_row(l, acc):
            old = vbuf[h, l]
            row = jnp.where(jnp.broadcast_to(lengths == l, old.shape), val_new, old)
            vbuf[h, l] = row
            return acc + s_ref[pl.ds(l, 1), :] * row.astype(jnp.float32)

        attn_ref[here, :] = lax.fori_loop(0, cache_len, mix_row, jnp.zeros((head_dim, batch), jnp.float32), unroll=4)
        v_out(h).start()
        return carry

    lax.fori_loop(0, heads, one_head, 0)
    attended = attn_ref[...].T.astype(jnp.bfloat16)
    wo_copy.wait()
    wide = 512
    for n in range(0, part_ref.shape[1], wide):
        part_ref[:, n:n + wide] = jnp.dot(attended, wobuf[:, n:n + wide], preferred_element_type=jnp.float32).astype(jnp.bfloat16)
    for h in range(heads):
        k_out(h).wait()
        v_out(h).wait()


def attend(new_hidden, cache_k, cache_v, lengths, ln1_gain, ln1_bias, w_q, w_k, w_v, w_o):
    batch, cache_len, heads, head_dim = cache_k.shape
    width = new_hidden.shape[1]
    flat = heads * head_dim
    rot_dim = head_dim // 2
    exponent = -2.0 * (np.arange(rot_dim) % (rot_dim // 2)) / rot_dim
    freqs = np.broadcast_to((ROPE_BASE ** exponent).astype(np.float32)[:, None], (rot_dim, batch))
    k_view = jnp.transpose(cache_k, (1, 2, 3, 0))
    v_view = jnp.transpose(cache_v, (1, 2, 3, 0))
    vmem = pl.BlockSpec(memory_space=pltpu.VMEM)
    hbm = pl.BlockSpec(memory_space=pl.ANY)
    cache_bytes = 8 * cache_k.size
    partial, k_new, v_new = pl.pallas_call(
        attention_kernel,
        out_shape=(
            jax.ShapeDtypeStruct((batch, width), jnp.bfloat16),
            jax.ShapeDtypeStruct(k_view.shape, jnp.bfloat16),
            jax.ShapeDtypeStruct(v_view.shape, jnp.bfloat16),
        ),
        in_specs=[vmem] * 5 + [hbm] * 6,
        out_specs=(vmem, hbm, hbm),
        scratch_shapes=[
            pltpu.VMEM((heads, cache_len, head_dim, batch), jnp.bfloat16),
            pltpu.VMEM((heads, cache_len, head_dim, batch), jnp.bfloat16),
            pltpu.VMEM((3, width, flat), jnp.bfloat16),
            pltpu.VMEM((flat, width), jnp.bfloat16),
            pltpu.VMEM((batch, width), jnp.bfloat16),
            pltpu.VMEM((3, flat, batch), jnp.float32),
            pltpu.VMEM((flat, batch), jnp.float32),
            pltpu.VMEM((flat, batch), jnp.float32),
            pltpu.VMEM((cache_len, batch), jnp.float32),
            pltpu.SemaphoreType.DMA((4,)),
            pltpu.SemaphoreType.DMA((heads,)),
            pltpu.SemaphoreType.DMA((heads,)),
            pltpu.SemaphoreType.DMA((heads,)),
            pltpu.SemaphoreType.DMA((heads,)),
        ],
        compiler_params=pltpu.CompilerParams(vmem_limit_bytes=VMEM_LIMIT),
        cost_estimate=pl.CostEstimate(flops=8 * batch * width * flat, bytes_accessed=cache_bytes + 8 * width * flat, transcendentals=0),
        name="attend",
    )(new_hidden, lengths[None, :], jnp.asarray(freqs), ln1_gain[None, :], ln1_bias[None, :], w_q, w_k, w_v, w_o, k_view, v_view)
    return partial, jnp.transpose(k_new, (3, 0, 1, 2)), jnp.transpose(v_new, (3, 0, 1, 2))


def reduce_to_all(partial, residual, ways):
    batch, width = partial.shape
    piece = width // ways
    received = lax.all_to_all(partial, 'tp', 1, 0, tiled=True)
    summed = jnp.sum(received.reshape(ways, batch, piece).astype(jnp.float32), axis=0)
    start = lax.axis_index('tp') * piece
    own_resid = lax.dynamic_slice_in_dim(residual, start, piece, axis=1)
    own_sum = (own_resid.astype(jnp.float32) + summed).astype(jnp.bfloat16)
    return lax.all_gather(own_sum, 'tp', axis=1, tiled=True)


def solution(mesh):
    ways = mesh.shape['tp']
    row_spec = P('bs', None)
    cache_spec = P('bs', None, 'tp', None)
    col_split = P(None, 'tp')
    row_split = P('tp', None)
    in_specs = (row_spec, cache_spec, cache_spec, P('bs'), P(), P(), col_split, col_split, col_split, row_split, P(), P(), col_split, row_split, P(), P(), col_split)
    out_specs = (P('bs', 'tp'), cache_spec, cache_spec, row_spec)

    def local_step(new_hidden, cache_k, cache_v, lengths, ln1_gain, ln1_bias, w_q, w_k, w_v, w_o, ln2_gain, ln2_bias, w_up, w_down, lnf_gain, lnf_bias, w_out):
        partial_o, new_cache_k, new_cache_v = attend(new_hidden, cache_k, cache_v, lengths, ln1_gain, ln1_bias, w_q, w_k, w_v, w_o)
        mid_hidden = reduce_to_all(partial_o, new_hidden, ways)
        normed_mid = norm_block(mid_hidden.astype(jnp.float32), ln2_gain, ln2_bias).astype(jnp.bfloat16)
        up_proj = jnp.dot(normed_mid, w_up, preferred_element_type=jnp.float32)
        activated = jnp.square(jnp.maximum(up_proj, 0.0)).astype(jnp.bfloat16)
        partial_m = jnp.dot(activated, w_down, preferred_element_type=jnp.float32).astype(jnp.bfloat16)
        out_hidden = reduce_to_all(partial_m, mid_hidden, ways)
        normed_out = norm_block(out_hidden.astype(jnp.float32), lnf_gain, lnf_bias).astype(jnp.bfloat16)
        logits = jnp.dot(normed_out, w_out, preferred_element_type=jnp.float32)
        local_peak = jnp.max(logits, axis=-1)
        local_total = jnp.sum(jnp.exp(logits - local_peak[:, None]), axis=-1)
        gathered = lax.all_gather(jnp.stack([local_peak, local_total]), 'tp')
        global_peak = jnp.max(gathered[:, 0], axis=0)
        global_total = jnp.sum(gathered[:, 1] * jnp.exp(gathered[:, 0] - global_peak[None, :]), axis=0)
        log_probs = logits - (global_peak + jnp.log(global_total))[:, None]
        return log_probs, new_cache_k, new_cache_v, out_hidden

    return jax.shard_map(local_step, mesh=mesh, in_specs=in_specs, out_specs=out_specs, check_vma=False)
```

time: 243 us -> 211 us (0.87)
  other arithmetic: 80.5 us -> 27.6 us
  Pallas kernels: 0 us -> 34.6 us
  matrix products: 58.8 us -> 46.8 us
    pallas_call x0 -> x1, Pallas kernels: none -> 34.6 us  [attend(): pl.pallas_call(attention_kernel, out_shape=(jax.ShapeDtypeStruct((batch,...]
    unnamed x3 -> x1, other arithmetic: 23.8 us -> 0.01 us
    dot_general x1 -> x0, other arithmetic: 21.6 us -> none  [project_and_attend(): jnp.einsum('bgrl,blgk->bgrk', attn_prob, new_cache_v, preferred_element_t...]
    dot_general x4 -> x0, matrix products: 10.9 us -> none  [the longest x1 4.09 us: project_and_attend(): jnp.dot(normed, w_k, preferred_element_type=jnp.float32)]
    reduce_sum x6 -> x4, other arithmetic: 10.3 us -> 6.95 us  [the longest x2 3.6 us: norm_block(): variance = jnp.mean(jnp.square(centered), axis=-1, keepdims=True)]
    unnamed x28 -> x13, local copies, waits for them, and re-layouts: 3.87 us -> 1.09 us
    broadcast_in_dim x0 -> x2, local copies, waits for them, and re-layouts: none -> 2.61 us  [the longest x1 1.31 us: attend(): ln1_gain[None, :]]
where the time goes in v1:
time: 211 us; the launch traced here: 210 us
  waiting for transfers between devices  48.4 us (23%)
  matrix products  46.8 us (22%)
  Pallas kernels  34.6 us (16%)
  other arithmetic  27.6 us (13%)
  blocking collectives  26.5 us (13%)
  between operations  14.2 us (7%)
  local copies, waits for them, and re-layouts  7.64 us (4%)
  starting transfers between devices  4.79 us (2%)
    pallas_call x1, Pallas kernels, attend(): pl.pallas_call(attention_kernel, out_shape=(jax.ShapeDtypeStruct((batch,...  34.6 us
    all_gather x2, waiting for transfers between devices, reduce_to_all(): return lax.all_gather(own_sum, 'tp', axis=1, tiled=True)  31.4 us
    dot_general x1, matrix products, local_step(): logits = jnp.dot(normed_out, w_out, preferred_element_type=jnp.float32)  31.3 us
    all_to_all x1, blocking collectives, reduce_to_all(): received = lax.all_to_all(partial, 'tp', 1, 0, tiled=True)  19.7 us
    all_to_all x1, waiting for transfers between devices, reduce_to_all(): received = lax.all_to_all(partial, 'tp', 1, 0, tiled=True)  17 us
    dot_general x1, matrix products, local_step(): jnp.dot(activated, w_down, preferred_element_type=jnp.float32)  15.4 us
    sub x1, other arithmetic, local_step(): log_probs = logits - (global_peak + jnp.log(global_total))[:, None]  10.9 us
    all_gather x1, blocking collectives, local_step(): gathered = lax.all_gather(jnp.stack([local_peak, local_total]), 'tp')  6.83 us
  transfers between devices with their start and end apart: 3, of which 3 were waited for; matrix products, arithmetic and copies ran while one was open for 0% of the time, Pallas kernels for 0%

profile of v1, /device:TPU:0, one launch (start us, length us, event | category | flops | bytes accessed | tf_op | source)
XLA Modules:
  0.0 210.5 jit_solution(16623382010214374521)
XLA Ops:
  7.2 1.3 broadcast_in_dim.7.gain_ref
  8.5 1.3 broadcast_in_dim.8.bias_ref
  9.8 1.3 jit_solution_.3.freq_ref
  11.1 34.6 %attend.1 = (bf16[256,2560]{1,0:T(8,128)(2,1)}, bf16[64,8,80,256]{3,2,1,0:T(8,128)(2,1)}, bf16[64,8,80,256]{3,2,1,0:T(8,128)(2,1)}) custom-call(bf16[256,2560]{1,0:T(8,128)(2,1)} %x_ref.1, s32[1,256]{1,0:T(1,128)} %bitcast.39, f32[40,256]{1,0:T(8,128)} %jit_solution_.3.freq_ref, f32[1,2560]{1,0:T(1,128)} %broadcast_in_dim.7.gain_ref, ...), custom_call_target="tpu_custom_call" | custom-call | flops 3355443200 | bytes 96993280 | tf_op jit(solution)/shard_map/attend/pallas_call | solution.py:142
  45.7 2.5 %copy.39 = bf16[32,4,8,640]{3,2,0,1:T(8,128)(2,1)} copy(bf16[32,4,8,640]{3,2,1,0:T(8,128)(2,1)} %bitcast.35) | data formatting | bytes 2621440 | tf_op jit(solution)/shard_map/all_to_all | solution.py:177
  48.2 4.7 %all-to-all-start = ((bf16[256,4,640]{2,0,1:T(8,128)(2,1)}), bf16[256,4,640]{2,0,1:T(8,128)(2,1)S(1)}, u32[]{:S(2)}, u32[]{:S(2)}) async-start(bf16[256,4,640]{2,0,1:T(8,128)(2,1)} %bitcast.31), calls=%async_computation | async-start | bytes 2621440 | tf_op jit(solution)/shard_map/all_to_all | solution.py:177
  53.0 17.0 %all-to-all-done = bf16[256,4,640]{2,0,1:T(8,128)(2,1)S(1)} async-done(((bf16[256,4,640]{2,0,1:T(8,128)(2,1)}), bf16[256,4,640]{2,0,1:T(8,128)(2,1)S(1)}, u32[]{:S(2)}, u32[]{:S(2)}) %all-to-all-start) | async-done | bytes 1310752 | tf_op jit(solution)/shard_map/all_to_all | solution.py:177
  70.0 0.2 convert_reduce_fusion.3
  70.2 1.8 add_convert_fusion.1
  72.1 16.1 %all-gather.5.cloned.1.call-done = bf16[256,2560]{1,0:T(8,128)(2,1)} async-done(((bf16[256,640]{1,0:T(8,128)(2,1)}), bf16[256,2560]{1,0:T(8,128)(2,1)}) %all-gather.5.cloned.1.call-update) | async-done | bytes 1310736 | tf_op jit(solution)/shard_map/all_gather | solution.py:182
  88.1 1.7 convert_reduce_fusion.1
  89.8 1.8 fusion.10
  91.6 15.4 %convolution_convert_fusion = bf16[256,2560]{1,0:T(8,128)(2,1)S(1)} fusion(bf16[2560,2560]{1,0:T(8,128)(2,1)} %param.31, bf16[2560,2560]{1,0:T(8,128)(2,1)} %param.30, bf16[256,2560]{1,0:T(8,128)(2,1)S(1)} %copy-done.1, f32[2560]{0:T(1024)S(1)} %copy-done.4, f32[2560]{0:T(1024)S(1)} %broadcast_add_fusion.1, f32[256]{0:T(256)S(1)} %add_rsqrt_fusion.1, ...), kind=kOutput, calls=%fused_computation.5 | convolution fusion | flops 6717440000 | bytes 28858368 | tf_op jit(solution)/shard_map/dot_general | solution.py:200
  107.2 19.7 %all_to_all.26 = bf16[256,4,640]{2,0,1:T(8,128)(2,1)S(1)} all-to-all(bf16[256,4,640]{2,0,1:T(8,128)(2,1)S(1)} %bitcast.34), channel_id=1, replica_groups=mesh['bs'=2,'tp'=4] {'tp'}, dimensions={1} | all-to-all | bytes 2621440 | tf_op jit(solution)/shard_map/all_to_all | solution.py:177
  126.9 0.2 convert_reduce_fusion.2
  127.1 0.8 add_convert_fusion
  128.0 15.3 %all-gather.7.cloned.1.call-done = bf16[256,2560]{1,0:T(8,128)(2,1)} async-done(((bf16[256,640]{1,0:T(8,128)(2,1)}), bf16[256,2560]{1,0:T(8,128)(2,1)}) %all-gather.7.cloned.1.call-update) | async-done | bytes 1310736 | tf_op jit(solution)/shard_map/all_gather | solution.py:182
  143.3 1.7 convert_reduce_fusion
  144.9 1.8 fusion.6
  146.8 31.3 %fusion.32 = (f32[256]{0:T(256)S(1)}, f32[256,12800]{1,0:T(8,128)}) fusion(bf16[2560,12800]{1,0:T(8,128)(2,1)} %param.34, bf16[256,2560]{1,0:T(8,128)(2,1)S(1)} %copy-done, f32[2560]{0:T(1024)S(1)} %copy-done.5, f32[2560]{0:T(1024)S(1)} %broadcast_add_fusion, f32[256]{0:T(256)S(1)} %add_rsqrt_fusion, f32[256]{0:T(256)S(1)} %broadcast_multiply_fusion), kind=kOutput, calls=%fused_computation.53 | convolution fusion | flops 16784424960 | bytes 79977472 | tf_op jit(solution)/shard_map/dot_general | solution.py:203
  178.1 6.6 %exponential_reduce_fusion = f32[256]{0:T(256)S(1)} fusion(f32[256,12800]{1,0:T(8,128)} %get-tuple-element.14, f32[256]{0:T(256)S(1)} %get-tuple-element.13), kind=kLoop, calls=%fused_computation | loop fusion | flops 6553344 | bytes 13109248 | tf_op jit(solution)/shard_map/reduce_sum | solution.py:205
  184.7 6.8 %all-gather.1 = f32[4,2,256]{2,1,0:T(2,128)S(1)} all-gather(f32[1,2,256]{2,1,0:T(2,128)S(1)} %maximum_bitcast_fusion), channel_id=2, replica_groups=mesh['bs'=2,'tp'=4] {'tp'}, dimensions={0}, use_global_device_ids=true | all-gather | bytes 10240 | tf_op jit(solution)/shard_map/all_gather | solution.py:206
  191.6 10.9 %broadcast_subtract_fusion = f32[256,12800]{1,0:T(8,128)} fusion(f32[256,12800]{1,0:T(8,128)} %get-tuple-element.14, f32[256]{0:T(256)S(1)} %log_add_fusion), kind=kLoop, calls=%fused_computation.1 | loop fusion | flops 3276800 | bytes 26215424 | tf_op jit(solution)/shard_map/sub | solution.py:209
  202.6 1.1 copy.41
  (27 shorter events, 0.3 us)
Async XLA Ops:
  48.2 23.8 %copy-start.2 = (f32[2560]{0:T(1024)S(1)}, f32[2560]{0:T(1024)}, u32[]{:S(2)}) copy-start(f32[2560]{0:T(1024)} %param.28) | copy-start | bytes 30724
  48.2 21.8 %all-to-all-start = ((bf16[256,4,640]{2,0,1:T(8,128)(2,1)}), bf16[256,4,640]{2,0,1:T(8,128)(2,1)S(1)}, u32[]{:S(2)}, u32[]{:S(2)}) async-start(bf16[256,4,640]{2,0,1:T(8,128)(2,1)} %bitcast.31), calls=%async_computation | async-start | bytes 2621440 | tf_op jit(solution)/shard_map/all_to_all | solution.py:177
  53.0 35.2 %all-gather.5.cloned.1.call-start = ((), (), s32[]{:S(2)}) async-start(), calls=%async_computation.2 | async-start | bytes 1638400 | tf_op jit(solution)/shard_map/all_gather | solution.py:182
  70.2 21.4 %copy-start.4 = (f32[2560]{0:T(1024)S(1)}, f32[2560]{0:T(1024)}, u32[]{:S(2)}) copy-start(f32[2560]{0:T(1024)} %param.29) | copy-start | bytes 30724
  72.0 71.3 %all-gather.7.cloned.1.call-start = ((), (), s32[]{:S(2)}) async-start(), calls=%async_computation.3 | async-start | bytes 1638400 | tf_op jit(solution)/shard_map/all_gather | solution.py:182
  88.1 3.5 %copy-start.1 = (bf16[256,2560]{1,0:T(8,128)(2,1)S(1)}, bf16[256,2560]{1,0:T(8,128)(2,1)}, u32[]{:S(2)}) copy-start(bf16[256,2560]{1,0:T(8,128)(2,1)} %all-gather.5.cloned.1.call-done) | copy-start | bytes 3932164
  107.2 20.7 %copy-start.3 = (f32[2560]{0:T(1024)S(1)}, f32[2560]{0:T(1024)}, u32[]{:S(2)}) copy-start(f32[2560]{0:T(1024)} %param.32) | copy-start | bytes 30724
  127.1 19.7 %copy-start.5 = (f32[2560]{0:T(1024)S(1)}, f32[2560]{0:T(1024)}, u32[]{:S(2)}) copy-start(f32[2560]{0:T(1024)} %param.33) | copy-start | bytes 30724
  143.3 3.5 %copy-start = (bf16[256,2560]{1,0:T(8,128)(2,1)S(1)}, bf16[256,2560]{1,0:T(8,128)(2,1)}, u32[]{:S(2)}) copy-start(bf16[256,2560]{1,0:T(8,128)(2,1)} %all-gather.7.cloned.1.call-done) | copy-start | bytes 3932164
Sparse Core Ops, SparseCore 0:
  72.1 15.9 all-gather.4
  128.1 15.1 all-gather.6

commit v2 on v1

--- a/solution.py
+++ b/solution.py
@@ -9,6 +9,9 @@
 EPSILON = 1e-5
 ROPE_BASE = 10000.0
 AHEAD = 2
+WIDE = 512
+SLOTS = 18
+EARLY = 14
 VMEM_LIMIT = 66 * 1000 * 1000
 
 
@@ -171,19 +174,275 @@
     return partial, jnp.transpose(k_new, (3, 0, 1, 2)), jnp.transpose(v_new, (3, 0, 1, 2))
 
 
-def reduce_to_all(partial, residual, ways):
+def layer_kernel(part_ref, x_hbm, gain2_hbm, bias2_hbm, gainf_hbm, biasf_hbm, up_hbm, down_hbm, out_hbm, y_ref, z_hbm, lse_ref, slots, recv, recv2, h2, act, part2, hf, x1, xrow, norms, zst, peak, total, stats, load_sem, slot_sem, zout_sem, send_sem, rs_sem, ag_sem, rs2_sem, agf_sem, agy_sem, st_sem):
+    batch, width = part_ref.shape
+    own_rows = x1.shape[0]
+    half = 2 * own_rows
+    count, _, wide = slots.shape
+    n_up = up_hbm.shape[1] // wide
+    n_down = down_hbm.shape[1] // wide
+    n_out = out_hbm.shape[1] // wide
+    first_out = n_up + n_down
+    me = lax.axis_index("tp")
+    chip = me // 2
+    core = lax.rem(me, 2)
+    partner = 2 * chip + 1 - core
+    cross = 2 * (1 - chip) + core
+    diag = 2 * (1 - chip) + 1 - core
+    local = pl.ds(pl.multiple_of(half * chip, half), half)
+    remote = pl.ds(pl.multiple_of(half * (1 - chip), half), half)
+
+    def rows_of(owner):
+        return pl.ds(pl.multiple_of(own_rows * owner, own_rows), own_rows)
+
+    def cols(n):
+        return pl.ds(pl.multiple_of(n * wide, wide), wide)
+
+    def push(src, dst, sem, recv_sem, to):
+        return pltpu.make_async_remote_copy(src_ref=src, dst_ref=dst, send_sem=sem, recv_sem=recv_sem, device_id={"tp": to}, device_id_type=pl.DeviceIdType.MESH)
+
+    def load_up(n):
+        return pltpu.make_async_copy(up_hbm.at[:, cols(n)], slots.at[n], slot_sem.at[n])
+
+    def load_down(n):
+        return pltpu.make_async_copy(down_hbm.at[:, cols(n)], slots.at[n_up + n], slot_sem.at[n_up + n])
+
+    def load_out(j):
+        slot = lax.rem(j + first_out, count)
+        return pltpu.make_async_copy(out_hbm.at[:, cols(j)], slots.at[slot], slot_sem.at[slot])
+
+    small = [pltpu.make_async_copy(x_hbm.at[rows_of(me), :], xrow, load_sem.at[0])]
+    for i, src in enumerate((gain2_hbm, bias2_hbm, gainf_hbm, biasf_hbm)):
+        small.append(pltpu.make_async_copy(src, norms.at[i], load_sem.at[i + 1]))
+    for copy in small:
+        copy.start()
+
+    barrier = pltpu.get_barrier_semaphore()
+    for other in (partner, cross, diag):
+        pl.semaphore_signal(barrier, inc=1, device_id={"tp": other}, device_id_type=pl.DeviceIdType.MESH)
+    pl.semaphore_wait(barrier, 3)
+
+    rs = [push(part_ref.at[rows_of(p), :], recv.at[me], send_sem.at[i], rs_sem.at[me], p) for i, p in enumerate((cross, diag, partner))]
+    for copy in rs:
+        copy.start()
+    for n in range(n_up):
+        load_up(n).start()
+    for n in range(n_down):
+        load_down(n).start()
+    for j in range(count - first_out):
+        load_out(j).start()
+    for copy in small:
+        copy.wait()
+
+    def arrived(ref, sem, owner):
+        pltpu.make_async_copy(ref, ref, sem.at[owner]).wait()
+
+    for p in (partner, cross, diag):
+        arrived(recv.at[p], rs_sem, p)
+    step = 16
+
+    def mid_rows(i, carry):
+        here = pl.ds(pl.multiple_of(i * step, step), step)
+        mine = pl.ds(pl.multiple_of(own_rows * me + i * step, step), step)
+        summed = part_ref[mine, :].astype(jnp.float32)
+        for p in (partner, cross, diag):
+            summed = summed + recv[p, here, :].astype(jnp.float32)
+        mid = (xrow[here, :].astype(jnp.float32) + summed).astype(jnp.bfloat16)
+        x1[here, :] = mid
+        h2[mine, :] = norm_block(mid.astype(jnp.float32), norms[0], norms[1]).astype(jnp.bfloat16)
+        return carry
+
+    lax.fori_loop(0, own_rows // step, mid_rows, 0)
+    own2 = h2.at[rows_of(me), :]
+    ag = [push(own2, own2, send_sem.at[3], ag_sem.at[me], cross), push(own2, own2, send_sem.at[4], ag_sem.at[me], partner)]
+    for copy in ag:
+        copy.start()
+
+    def mlp_up(rows):
+        def body(n, carry):
+            up = jnp.dot(h2[rows, :], slots[n], preferred_element_type=jnp.float32)
+            act[:, cols(n)] = jnp.square(jnp.maximum(up, 0.0)).astype(jnp.bfloat16)
+            return carry
+
+        lax.fori_loop(0, n_up, body, 0)
+
+    def down_block(rows, n):
+        part2[rows, cols(n)] = jnp.dot(act[...], slots[n_up + n], preferred_element_type=jnp.float32).astype(jnp.bfloat16)
+
+    arrived(h2.at[rows_of(partner), :], ag_sem, partner)
+    for n in range(n_up):
+        load_up(n).wait()
+    mlp_up(local)
+    for n in range(n_down):
+        load_down(n).wait()
+
+    def down_local(n, carry):
+        down_block(local, n)
+        return carry
+
+    lax.fori_loop(0, n_down, down_local, 0)
+    to_partner = push(part2.at[rows_of(partner), :], recv2.at[me], send_sem.at[5], rs2_sem.at[me], partner)
+    to_partner.start()
+    arrived(h2.at[rows_of(cross), :], ag_sem, cross)
+    relay2 = push(h2.at[rows_of(cross), :], h2.at[rows_of(cross), :], send_sem.at[6], ag_sem.at[cross], partner)
+    relay2.start()
+    arrived(h2.at[rows_of(diag), :], ag_sem, diag)
+    mlp_up(remote)
+    for j in range(count - first_out, count - n_down):
+        load_out(j).start()
+
+    def down_remote(n, carry):
+        down_block(remote, n)
+        for i, p in enumerate((cross, diag)):
+            push(part2.at[rows_of(p), cols(n)], recv2.at[me, :, cols(n)], send_sem.at[7 + i], rs2_sem.at[me], p).start()
+        return carry
+
+    lax.fori_loop(0, n_down, down_remote, 0)
+    for j in range(count - n_down, count):
+        load_out(j).start()
+
+    for p in (partner, cross, diag):
+        arrived(recv2.at[p], rs2_sem, p)
+
+    def out_rows(i, carry):
+        here = pl.ds(pl.multiple_of(i * step, step), step)
+        mine = pl.ds(pl.multiple_of(own_rows * me + i * step, step), step)
+        summed = part2[mine, :].astype(jnp.float32)
+        for p in (partner, cross, diag):
+            summed = summed + recv2[p, here, :].astype(jnp.float32)
+        out = (x1[here, :].astype(jnp.float32) + summed).astype(jnp.bfloat16)
+        y_ref[mine, :] = out
+        hf[mine, :] = norm_block(out.astype(jnp.float32), norms[2], norms[3]).astype(jnp.bfloat16)
+        return carry
+
+    lax.fori_loop(0, own_rows // step, out_rows, 0)
+    ownf = hf.at[rows_of(me), :]
+    owny = y_ref.at[rows_of(me), :]
+    agf = [push(ownf, ownf, send_sem.at[9], agf_sem.at[me], cross), push(ownf, ownf, send_sem.at[10], agf_sem.at[me], partner)]
+    agy = [push(owny, owny, send_sem.at[11], agy_sem.at[me], cross), push(owny, owny, send_sem.at[12], agy_sem.at[me], partner)]
+    for copy in agf + agy:
+        copy.start()
+
+    peak[...] = jnp.full(peak.shape, -jnp.inf, jnp.float32)
+    total[...] = jnp.zeros(total.shape, jnp.float32)
+    lanes = peak.shape[1]
+
+    def head_block(rows, j, buf):
+        z = jnp.dot(hf[rows, :], slots[lax.rem(j + first_out, count)], preferred_element_type=jnp.float32)
+        buf[...] = z
+        pieces = [z[:, c:c + lanes] for c in range(0, wide, lanes)]
+        old = peak[rows, :]
+        new = old
+        for piece in pieces:
+            new = jnp.maximum(new, piece)
+        acc = total[rows, :] * jnp.exp(old - new)
+        for piece in pieces:
+            acc = acc + jnp.exp(piece - new)
+        peak[rows, :] = new
+        total[rows, :] = acc
+
+    def head_loop(rows, size, lo, hi, before, after):
+        def copy_z(j):
+            turn = lax.rem(j, 2)
+            return pltpu.make_async_copy(zst.at[turn, pl.ds(0, size), :], z_hbm.at[rows, cols(j)], zout_sem.at[turn])
+
+        def body(j, carry):
+            before(j)
+
+            @pl.when(j >= lo + 2)
+            def _():
+                copy_z(j - 2).wait()
+
+            head_block(rows, j, zst.at[lax.rem(j, 2), pl.ds(0, size), :])
+            copy_z(j).start()
+            after(j)
+            return carry
+
+        lax.fori_loop(lo, hi, body, 0)
+        for j in range(hi - 2, hi):
+            copy_z(j).wait()
+
+    def nothing(j):
+        pass
+
+    def next_out(j):
+        @pl.when(j + count < n_out)
+        def _():
+            load_out(j + count).start()
+
+    arrived(hf.at[rows_of(partner), :], agf_sem, partner)
+    head_loop(local, half, 0, EARLY, lambda j: load_out(j).wait(), nothing)
+    arrived(hf.at[rows_of(cross), :], agf_sem, cross)
+    relayf = push(hf.at[rows_of(cross), :], hf.at[rows_of(cross), :], send_sem.at[13], agf_sem.at[cross], partner)
+    relayf.start()
+    arrived(hf.at[rows_of(diag), :], agf_sem, diag)
+    head_loop(remote, half, 0, EARLY, nothing, next_out)
+    arrived(y_ref.at[rows_of(cross), :], agy_sem, cross)
+    relayy = push(y_ref.at[rows_of(cross), :], y_ref.at[rows_of(cross), :], send_sem.at[14], agy_sem.at[cross], partner)
+    relayy.start()
+    head_loop(pl.ds(0, batch), batch, EARLY, n_out, lambda j: load_out(j).wait(), next_out)
+
+    top = jnp.max(peak[...], axis=1, keepdims=True)
+    bottom = jnp.sum(total[...] * jnp.exp(peak[...] - top), axis=1, keepdims=True)
+    stats[me, 0] = jnp.broadcast_to(top, peak.shape).T[0:8]
+    stats[me, 1] = jnp.broadcast_to(bottom, peak.shape).T[0:8]
+    st = [push(stats.at[me], stats.at[me], send_sem.at[15 + i], st_sem.at[me], p) for i, p in enumerate((cross, diag, partner))]
+    for copy in st:
+        copy.start()
+    for p in (partner, diag):
+        arrived(y_ref.at[rows_of(p), :], agy_sem, p)
+    for p in (partner, cross, diag):
+        arrived(stats.at[p], st_sem, p)
+    tops = [stats[i, 0] for i in range(4)]
+    whole_top = jnp.maximum(jnp.maximum(tops[0], tops[1]), jnp.maximum(tops[2], tops[3]))
+    whole = sum(stats[i, 1] * jnp.exp(tops[i] - whole_top) for i in range(4))
+    lse = whole_top + jnp.log(whole)
+    lse_ref[...] = jnp.broadcast_to(lse[0:1], (lanes, batch)).T
+
+    for copy in rs + ag + [to_partner, relay2] + agf + agy + [relayf, relayy] + st:
+        copy.wait_send()
+    for i, p in enumerate((cross, diag)):
+        push(part2.at[rows_of(p), :], recv2.at[me], send_sem.at[7 + i], rs2_sem.at[me], p).wait_send()
+
+
+def finish_layer(partial, new_hidden, ln2_gain, ln2_bias, lnf_gain, lnf_bias, w_up, w_down, w_out):
     batch, width = partial.shape
-    piece = width // ways
-    received = lax.all_to_all(partial, 'tp', 1, 0, tiled=True)
-    summed = jnp.sum(received.reshape(ways, batch, piece).astype(jnp.float32), axis=0)
-    start = lax.axis_index('tp') * piece
-    own_resid = lax.dynamic_slice_in_dim(residual, start, piece, axis=1)
-    own_sum = (own_resid.astype(jnp.float32) + summed).astype(jnp.bfloat16)
-    return lax.all_gather(own_sum, 'tp', axis=1, tiled=True)
+    own_rows = batch // 4
+    vocab = w_out.shape[1]
+    vmem = pl.BlockSpec(memory_space=pltpu.VMEM)
+    hbm = pl.BlockSpec(memory_space=pl.ANY)
+    dma = pltpu.SemaphoreType.DMA
+    bf16, f32 = jnp.bfloat16, jnp.float32
+    hidden, logits, lse = pl.pallas_call(
+        layer_kernel,
+        out_shape=(jax.ShapeDtypeStruct((batch, width), bf16), jax.ShapeDtypeStruct((batch, vocab), f32), jax.ShapeDtypeStruct((batch, 128), f32)),
+        in_specs=[vmem] + [hbm] * 8,
+        out_specs=(vmem, hbm, vmem),
+        scratch_shapes=[
+            pltpu.VMEM((SLOTS, width, WIDE), bf16),
+            pltpu.VMEM((4, own_rows, width), bf16),
+            pltpu.VMEM((4, own_rows, width), bf16),
+            pltpu.VMEM((batch, width), bf16),
+            pltpu.VMEM((2 * own_rows, w_up.shape[1]), bf16),
+            pltpu.VMEM((batch, width), bf16),
+            pltpu.VMEM((batch, width), bf16),
+            pltpu.VMEM((own_rows, width), bf16),
+            pltpu.VMEM((own_rows, width), bf16),
+            pltpu.VMEM((4, 1, width), f32),
+            pltpu.VMEM((2, batch, WIDE), f32),
+            pltpu.VMEM((batch, 128), f32),
+            pltpu.VMEM((batch, 128), f32),
+            pltpu.VMEM((4, 2, 8, batch), f32),
+            dma((5,)), dma((SLOTS,)), dma((2,)), dma((18,)), dma((4,)), dma((4,)), dma((4,)), dma((4,)), dma((4,)), dma((4,)),
+        ],
+        compiler_params=pltpu.CompilerParams(vmem_limit_bytes=VMEM_LIMIT, collective_id=0, has_side_effects=True),
+        cost_estimate=pl.CostEstimate(flops=2 * batch * (w_up.size + w_down.size + w_out.size), bytes_accessed=2 * (w_up.size + w_down.size + w_out.size), transcendentals=batch * vocab),
+        name="layer",
+    )(partial, new_hidden, ln2_gain[None, :], ln2_bias[None, :], lnf_gain[None, :], lnf_bias[None, :], w_up, w_down, w_out)
+    return hidden, logits - lse[:, :1]
 
 
 def solution(mesh):
-    ways = mesh.shape['tp']
     row_spec = P('bs', None)
     cache_spec = P('bs', None, 'tp', None)
     col_split = P(None, 'tp')
@@ -193,20 +452,7 @@
 
     def local_step(new_hidden, cache_k, cache_v, lengths, ln1_gain, ln1_bias, w_q, w_k, w_v, w_o, ln2_gain, ln2_bias, w_up, w_down, lnf_gain, lnf_bias, w_out):
         partial_o, new_cache_k, new_cache_v = attend(new_hidden, cache_k, cache_v, lengths, ln1_gain, ln1_bias, w_q, w_k, w_v, w_o)
-        mid_hidden = reduce_to_all(partial_o, new_hidden, ways)
-        normed_mid = norm_block(mid_hidden.astype(jnp.float32), ln2_gain, ln2_bias).astype(jnp.bfloat16)
-        up_proj = jnp.dot(normed_mid, w_up, preferred_element_type=jnp.float32)
-        activated = jnp.square(jnp.maximum(up_proj, 0.0)).astype(jnp.bfloat16)
-        partial_m = jnp.dot(activated, w_down, preferred_element_type=jnp.float32).astype(jnp.bfloat16)
-        out_hidden = reduce_to_all(partial_m, mid_hidden, ways)
-        normed_out = norm_block(out_hidden.astype(jnp.float32), lnf_gain, lnf_bias).astype(jnp.bfloat16)
-        logits = jnp.dot(normed_out, w_out, preferred_element_type=jnp.float32)
-        local_peak = jnp.max(logits, axis=-1)
-        local_total = jnp.sum(jnp.exp(logits - local_peak[:, None]), axis=-1)
-        gathered = lax.all_gather(jnp.stack([local_peak, local_total]), 'tp')
-        global_peak = jnp.max(gathered[:, 0], axis=0)
-        global_total = jnp.sum(gathered[:, 1] * jnp.exp(gathered[:, 0] - global_peak[None, :]), axis=0)
-        log_probs = logits - (global_peak + jnp.log(global_total))[:, None]
+        out_hidden, log_probs = finish_layer(partial_o, new_hidden, ln2_gain, ln2_bias, lnf_gain, lnf_bias, w_up, w_down, w_out)
         return log_probs, new_cache_k, new_cache_v, out_hidden
 
     return jax.shard_map(local_step, mesh=mesh, in_specs=in_specs, out_specs=out_specs, check_vma=False)

time: 211 us -> 147 us (0.70)
  Pallas kernels: 34.6 us -> 124 us
  waiting for transfers between devices: 48.4 us -> 0 us
  matrix products: 46.8 us -> 0 us
  blocking collectives: 26.5 us -> 0 us
  other arithmetic: 27.6 us -> 11 us
  between operations: 14.2 us -> 0.66 us
  starting transfers between devices: 4.79 us -> 0 us
  local copies, waits for them, and re-layouts: 7.64 us -> 11.3 us
    pallas_call x0 -> x1, Pallas kernels: none -> 89 us  [finish_layer(): pl.pallas_call(layer_kernel, out_shape=(jax.ShapeDtypeStruct((batch, widt...]
    dot_general x2 -> x0, matrix products: 46.8 us -> none  [the longest x1 31.3 us: local_step(): logits = jnp.dot(normed_out, w_out, preferred_element_type=jnp.float32)]
    all_gather x2 -> x0, waiting for transfers between devices: 31.4 us -> none  [reduce_to_all(): return lax.all_gather(own_sum, 'tp', axis=1, tiled=True)]
    all_to_all x1 -> x0, blocking collectives: 19.7 us -> none  [reduce_to_all(): received = lax.all_to_all(partial, 'tp', 1, 0, tiled=True)]
    all_to_all x1 -> x0, waiting for transfers between devices: 17 us -> none  [reduce_to_all(): received = lax.all_to_all(partial, 'tp', 1, 0, tiled=True)]
    reduce_sum x8 -> x0, other arithmetic: 13.9 us -> none  [the longest x1 6.61 us: local_step(): local_total = jnp.sum(jnp.exp(logits - local_peak[:, None]), axis=-1)]
    all_gather x1 -> x0, blocking collectives: 6.83 us -> none  [local_step(): gathered = lax.all_gather(jnp.stack([local_peak, local_total]), 'tp')]
    broadcast_in_dim x0 -> x4, local copies, waits for them, and re-layouts: none -> 5.23 us  [the longest x1 1.31 us: finish_layer(): ln2_bias[None, :]]
  transfers between devices with their start and end apart: 3 -> 0, of which waited for: 3 -> 0; matrix products, arithmetic and copies ran while one was open for 0% -> 0% of each run, Pallas kernels for 0% -> 0%
where the time goes in v2:
time: 147 us
  Pallas kernels  124 us (84%)
  local copies, waits for them, and re-layouts  11.3 us (8%)
  other arithmetic  11 us (7%)
    pallas_call x1, Pallas kernels, finish_layer(): pl.pallas_call(layer_kernel, out_shape=(jax.ShapeDtypeStruct((batch, widt...  89 us
    pallas_call x1, Pallas kernels, attend(): pl.pallas_call(attention_kernel, out_shape=(jax.ShapeDtypeStruct((batch,...  34.6 us
    sub x1, other arithmetic, finish_layer(): return (hidden, logits - lse[:, :1])  11 us

profile of v2, /device:TPU:0, one launch (start us, length us, event | category | flops | bytes accessed | tf_op | source)
XLA Modules:
  0.0 146.6 jit_solution(15137834371187077228)
XLA Ops:
  0.6 1.3 broadcast_in_dim.22.gain_ref
  1.9 1.3 broadcast_in_dim.23.bias_ref
  3.2 1.3 broadcast_in_dim.24.gain2_hbm
  4.6 1.3 broadcast_in_dim.25.bias2_hbm
  5.9 1.3 broadcast_in_dim.26.gainf_hbm
  7.2 1.3 broadcast_in_dim.27.biasf_hbm
  8.5 1.3 jit_solution_.3.freq_ref
  9.8 34.6 %attend.1 = (bf16[256,2560]{1,0:T(8,128)(2,1)}, bf16[64,8,80,256]{3,2,1,0:T(8,128)(2,1)}, bf16[64,8,80,256]{3,2,1,0:T(8,128)(2,1)}) custom-call(bf16[256,2560]{1,0:T(8,128)(2,1)} %x_hbm.1, s32[1,256]{1,0:T(1,128)} %bitcast.7, f32[40,256]{1,0:T(8,128)} %jit_solution_.3.freq_ref, f32[1,2560]{1,0:T(1,128)} %broadcast_in_dim.22.gain_ref, ...), custom_call_target="tpu_custom_call" | custom-call | flops 3355443200 | bytes 96993280 | tf_op jit(solution)/shard_map/attend/pallas_call | solution.py:145
  44.4 89.0 %layer.1 = (bf16[256,2560]{1,0:T(8,128)(2,1)}, f32[256,12800]{1,0:T(8,128)}, f32[256,128]{1,0:T(8,128)}) custom-call(bf16[256,2560]{1,0:T(8,128)(2,1)} %get-tuple-element.10.part_ref, bf16[256,2560]{1,0:T(8,128)(2,1)} %x_hbm.1, f32[1,2560]{1,0:T(1,128)} %broadcast_in_dim.24.gain2_hbm, f32[1,2560]{1,0:T(1,128)} %broadcast_in_dim.25.bias2_hbm, ...), custom_call_target="tpu_custom_call" | custom-call | flops 23488102400 | bytes 91750400 | tf_op jit(solution)/shard_map/layer/pallas_call | solution.py:416
  133.4 1.0 slice_reduce_fusion
  134.5 0.0 copy-start
  134.5 11.0 %broadcast_subtract_fusion = f32[256,12800]{1,0:T(8,128)} fusion(f32[256,12800]{1,0:T(8,128)} %get-tuple-element.11, f32[256]{0:T(256)S(1)} %slice_reduce_fusion), kind=kLoop, calls=%fused_computation | loop fusion | flops 3276800 | bytes 26215424 | tf_op jit(solution)/shard_map/sub | solution.py:442
  145.5 0.0 copy-done
  145.5 1.1 copy.23
Async XLA Ops:
  134.5 11.1 %copy-start = (bf16[256,2560]{1,0:T(8,128)(2,1)S(1)}, bf16[256,2560]{1,0:T(8,128)(2,1)}, u32[]{:S(2)}) copy-start(bf16[256,2560]{1,0:T(8,128)(2,1)} %get-tuple-element.23) | copy-start | bytes 3932164

commit v3 on v2

v3 whole, which is shorter than its diff:
```python
import math
import jax
import jax.numpy as jnp
from jax import lax
from jax.experimental import pallas as pl
from jax.experimental.pallas import tpu as pltpu
from jax.sharding import PartitionSpec as P

EPSILON = 1e-5
ROPE_BASE = 10000.0
AHEAD_FAR = 6
AHEAD_NEAR = 3
WIDE = 512
SLOTS = 18
EARLY = 14
RELAY = 11
VMEM_LIMIT = 66 * 1000 * 1000


def norm_block(values, gain, bias):
    mean = jnp.mean(values, axis=-1, keepdims=True)
    centered = values - mean
    variance = jnp.mean(jnp.square(centered), axis=-1, keepdims=True)
    return centered * lax.rsqrt(variance + EPSILON) * (1.0 + gain) + bias


def attend_lanes(start, ahead, lengths, project, part, kc_hbm, vc_hbm, ko_hbm, vo_hbm, kbuf, vbuf, attn_ref, s_ref, ki_sem, vi_sem, ko_sem, vo_sem):
    heads, cache_len, head_dim, batch = kbuf.shape
    lanes = pl.ds(pl.multiple_of(start, batch), batch)

    def k_in(h):
        return pltpu.make_async_copy(kc_hbm.at[:, h, :, lanes], kbuf.at[h], ki_sem.at[h])

    def v_in(h):
        return pltpu.make_async_copy(vc_hbm.at[:, h, :, lanes], vbuf.at[h], vi_sem.at[h])

    def k_out(h):
        return pltpu.make_async_copy(kbuf.at[h], ko_hbm.at[:, h, :, lanes], ko_sem.at[h])

    def v_out(h):
        return pltpu.make_async_copy(vbuf.at[h], vo_hbm.at[:, h, :, lanes], vo_sem.at[h])

    for h in range(ahead):
        k_in(h).start()
        v_in(h).start()
    qkv = project()
    scale = head_dim ** -0.5

    def one_head(h, carry):
        @pl.when(h + ahead < heads)
        def _():
            k_in(h + ahead).start()
            v_in(h + ahead).start()

        here = pl.ds(pl.multiple_of(h * head_dim, head_dim), head_dim)
        query = qkv[0, here, :].astype(jnp.bfloat16).astype(jnp.float32)
        key_new = qkv[1, here, :].astype(jnp.bfloat16)
        val_new = qkv[2, here, :].astype(jnp.bfloat16)
        k_in(h).wait()

        def score_row(l, c):
            old = kbuf[h, l]
            row = jnp.where(jnp.broadcast_to(lengths == l, old.shape), key_new, old)
            kbuf[h, l] = row
            s_ref[pl.ds(l, 1), :] = jnp.sum(row.astype(jnp.float32) * query, axis=0, keepdims=True)
            return c

        lax.fori_loop(0, cache_len, score_row, 0, unroll=8)
        k_out(h).start()
        scores = s_ref[...] * scale
        valid = lax.broadcasted_iota(jnp.int32, scores.shape, 0) <= lengths
        scores = jnp.where(valid, scores, -1e30)
        weights = jnp.exp(scores - jnp.max(scores, axis=0, keepdims=True))
        s_ref[...] = (weights / jnp.sum(weights, axis=0, keepdims=True)).astype(jnp.bfloat16).astype(jnp.float32)
        v_in(h).wait()

        def mix_row(l, acc):
            old = vbuf[h, l]
            row = jnp.where(jnp.broadcast_to(lengths == l, old.shape), val_new, old)
            vbuf[h, l] = row
            return acc + s_ref[pl.ds(l, 1), :] * row.astype(jnp.float32)

        attn_ref[here, :] = lax.fori_loop(0, cache_len, mix_row, jnp.zeros((head_dim, batch), jnp.float32), unroll=8)
        v_out(h).start()
        return carry

    lax.fori_loop(0, heads, one_head, 0)
    part(attn_ref[...].T.astype(jnp.bfloat16))
    for h in range(heads):
        k_out(h).wait()
        v_out(h).wait()


def far_kernel(x_ref, len_ref, gain_ref, bias_ref, wq_hbm, wk_hbm, wv_hbm, wo_hbm, kc_hbm, vc_hbm, cross_ref, diag_ref, near_ref, ko_hbm, vo_hbm, kbuf, vbuf, wbuf, wobuf, h_ref, qkv_ref, tmp_ref, attn_ref, s_ref, far_ref, w_sem, ki_sem, vi_sem, ko_sem, vo_sem):
    heads, cache_len, head_dim, half = kbuf.shape
    batch = x_ref.shape[0]
    half_rot = head_dim // 4
    me = lax.axis_index("tp")
    chip = me // 2
    core = lax.rem(me, 2)
    copies = [pltpu.make_async_copy(src, wbuf.at[i], w_sem.at[i]) for i, src in enumerate((wq_hbm, wk_hbm, wv_hbm))]
    wo_copy = pltpu.make_async_copy(wo_hbm, wobuf, w_sem.at[3])
    for copy in copies:
        copy.start()
    rows = 32
    gain, bias = gain_ref[...][None, :], bias_ref[...][None, :]

    def project():
        def norm_rows(i, carry):
            here = pl.ds(pl.multiple_of(i * rows, rows), rows)
            h_ref[here, :] = norm_block(x_ref[here, :].astype(jnp.float32), gain, bias).astype(jnp.bfloat16)
            return carry

        lax.fori_loop(0, batch // rows, norm_rows, 0)
        index = lax.broadcasted_iota(jnp.int32, (2 * half_rot, batch), 0)
        upper = index < half_rot
        pair = jnp.where(upper, index, index - half_rot).astype(jnp.float32)
        angles = jnp.exp(pair * (-math.log(ROPE_BASE) / half_rot)) * len_ref[...].astype(jnp.float32)
        cosine = jnp.cos(angles)
        sine = jnp.where(upper, -jnp.sin(angles), jnp.sin(angles))
        for i in range(3):
            copies[i].wait()
            tmp_ref[...] = jnp.dot(h_ref[...], wbuf[i], preferred_element_type=jnp.float32).T
            for h in range(heads):
                base = h * head_dim
                if i == 2:
                    blocks = [(base, head_dim, tmp_ref[pl.ds(base, head_dim), :])]
                else:
                    first = tmp_ref[pl.ds(base, half_rot), :]
                    second = tmp_ref[pl.ds(base + half_rot, half_rot), :]
                    both = tmp_ref[pl.ds(base, 2 * half_rot), :]
                    swapped = jnp.concatenate([second, first], axis=0)
                    rest = head_dim - 2 * half_rot
                    blocks = [(base, 2 * half_rot, both * cosine + swapped * sine), (base + 2 * half_rot, rest, tmp_ref[pl.ds(base + 2 * half_rot, rest), :])]
                for at, size, value in blocks:
                    qkv_ref[0, i, pl.ds(at, size), :] = value[:, :half]
                    qkv_ref[1, i, pl.ds(at, size), :] = value[:, half:]
        wo_copy.start()
        near_ref[...] = qkv_ref[chip]
        return qkv_ref.at[1 - chip]

    def part(attended):
        wo_copy.wait()
        wide = 512
        for n in range(0, far_ref.shape[1], wide):
            far_ref[:, n:n + wide] = jnp.dot(attended, wobuf[:, n:n + wide], preferred_element_type=jnp.float32).astype(jnp.bfloat16)
        own = half // 2
        cross_ref[...] = far_ref[pl.ds(pl.multiple_of(own * core, own), own), :]
        diag_ref[...] = far_ref[pl.ds(pl.multiple_of(own * (1 - core), own), own), :]

    start = half * (1 - chip)
    lengths = len_ref[:, pl.ds(pl.multiple_of(start, half), half)]
    attend_lanes(start, AHEAD_FAR, lengths, project, part, kc_hbm, vc_hbm, ko_hbm, vo_hbm, kbuf, vbuf, attn_ref, s_ref, ki_sem, vi_sem, ko_sem, vo_sem)


def near_kernel(len_ref, qkv_ref, wo_hbm, kc_hbm, vc_hbm, ko_in, vo_in, part_ref, ko_hbm, vo_hbm, kbuf, vbuf, wobuf, attn_ref, s_ref, w_sem, ki_sem, vi_sem, ko_sem, vo_sem):
    half = kbuf.shape[3]
    chip = lax.axis_index("tp") // 2
    start = half * chip
    lengths = len_ref[:, pl.ds(pl.multiple_of(start, half), half)]
    wo_copy = pltpu.make_async_copy(wo_hbm, wobuf, w_sem.at[0])

    def project():
        wo_copy.start()
        return qkv_ref

    def part(attended):
        wo_copy.wait()
        wide = 512
        for n in range(0, part_ref.shape[1], wide):
            part_ref[:, n:n + wide] = jnp.dot(attended, wobuf[:, n:n + wide], preferred_element_type=jnp.float32).astype(jnp.bfloat16)

    attend_lanes(start, AHEAD_NEAR, lengths, project, part, kc_hbm, vc_hbm, ko_hbm, vo_hbm, kbuf, vbuf, attn_ref, s_ref, ki_sem, vi_sem, ko_sem, vo_sem)


def attend(new_hidden, cache_k, cache_v, lengths, ln1_gain, ln1_bias, w_q, w_k, w_v, w_o):
    batch, cache_len, heads, head_dim = cache_k.shape
    width = new_hidden.shape[1]
    flat = heads * head_dim
    half = batch // 2
    k_view = jnp.transpose(cache_k, (1, 2, 3, 0))
    v_view = jnp.transpose(cache_v, (1, 2, 3, 0))
    vmem = pl.BlockSpec(memory_space=pltpu.VMEM)
    hbm = pl.BlockSpec(memory_space=pl.ANY)
    dma = pltpu.SemaphoreType.DMA
    bf16, f32 = jnp.bfloat16, jnp.float32
    shape = jax.ShapeDtypeStruct
    lens = lengths[None, :]
    slabs = [pltpu.VMEM((heads, cache_len, head_dim, half), bf16)] * 2
    sems = [dma((heads,))] * 4
    to_cross, to_diag, near, k_half, v_half = pl.pallas_call(
        far_kernel,
        out_shape=(shape((half // 2, width), bf16), shape((half // 2, width), bf16), shape((3, flat, half), f32), shape(k_view.shape, bf16), shape(v_view.shape, bf16)),
        in_specs=[vmem] * 4 + [hbm] * 6,
        out_specs=(vmem, vmem, vmem, hbm, hbm),
        scratch_shapes=slabs + [
            pltpu.VMEM((3, width, flat), bf16),
            pltpu.VMEM((flat, width), bf16),
            pltpu.VMEM((batch, width), bf16),
            pltpu.VMEM((2, 3, flat, half), f32),
            pltpu.VMEM((flat, batch), f32),
            pltpu.VMEM((flat, half), f32),
            pltpu.VMEM((cache_len, half), f32),
            pltpu.VMEM((half, width), bf16),
            dma((4,)),
        ] + sems,
        compiler_params=pltpu.CompilerParams(vmem_limit_bytes=VMEM_LIMIT),
        cost_estimate=pl.CostEstimate(flops=8 * batch * width * flat, bytes_accessed=4 * cache_k.size + 8 * width * flat, transcendentals=0),
        name="far",
    )(new_hidden, lens, ln1_gain, ln1_bias, w_q, w_k, w_v, w_o, k_view, v_view)
    from_cross = lax.ppermute(to_cross, "tp", [(i, (i + 2) % 4) for i in range(4)])
    from_diag = lax.ppermute(to_diag, "tp", [(i, 3 - i) for i in range(4)])
    partial, k_new, v_new = pl.pallas_call(
        near_kernel,
        out_shape=(shape((half, width), bf16), shape(k_view.shape, bf16), shape(v_view.shape, bf16)),
        in_specs=[vmem] * 2 + [hbm] * 5,
        out_specs=(vmem, hbm, hbm),
        input_output_aliases={5: 1, 6: 2},
        scratch_shapes=slabs + [
            pltpu.VMEM((flat, width), bf16),
            pltpu.VMEM((flat, half), f32),
            pltpu.VMEM((cache_len, half), f32),
            dma((1,)),
        ] + sems,
        compiler_params=pltpu.CompilerParams(vmem_limit_bytes=VMEM_LIMIT),
        cost_estimate=pl.CostEstimate(flops=40 * batch * width * flat, bytes_accessed=4 * cache_k.size, transcendentals=0),
        name="near",
    )(lens, near, w_o, k_view, v_view, k_half, v_half)
    return (partial, from_cross, from_diag), jnp.transpose(k_new, (3, 0, 1, 2)), jnp.transpose(v_new, (3, 0, 1, 2))


def layer_kernel(near_ref, cross_ref, diag_ref, x_hbm, gain2_hbm, bias2_hbm, gainf_hbm, biasf_hbm, up_hbm, down_hbm, out_hbm, y_ref, z_hbm, lse_ref, slots, recv, recv2, h2, act, part2, hf, x1, xrow, norms, zst, peak, total, stats, load_sem, slot_sem, zout_sem, send_sem, rs_sem, ag_sem, rs2_sem, agf_sem, agy_sem, st_sem):
    batch, width = y_ref.shape
    own_rows = x1.shape[0]
    half = 2 * own_rows
    count, _, wide = slots.shape
    n_up = up_hbm.shape[1] // wide
    n_down = down_hbm.shape[1] // wide
    n_out = out_hbm.shape[1] // wide
    first_out = n_up + n_down
    me = lax.axis_index("tp")
    chip = me // 2
    core = lax.rem(me, 2)
    partner = 2 * chip + 1 - core
    cross = 2 * (1 - chip) + core
    diag = 2 * (1 - chip) + 1 - core
    local = pl.ds(pl.multiple_of(half * chip, half), half)
    remote = pl.ds(pl.multiple_of(half * (1 - chip), half), half)

    def rows_of(owner):
        return pl.ds(pl.multiple_of(own_rows * owner, own_rows), own_rows)

    def cols(n):
        return pl.ds(pl.multiple_of(n * wide, wide), wide)

    def push(src, dst, sem, recv_sem, to):
        return pltpu.make_async_remote_copy(src_ref=src, dst_ref=dst, send_sem=sem, recv_sem=recv_sem, device_id={"tp": to}, device_id_type=pl.DeviceIdType.MESH)

    def load_up(n):
        return pltpu.make_async_copy(up_hbm.at[:, cols(n)], slots.at[n], slot_sem.at[n])

    def load_down(n):
        return pltpu.make_async_copy(down_hbm.at[:, cols(n)], slots.at[n_up + n], slot_sem.at[n_up + n])

    def load_out(j):
        slot = lax.rem(j + first_out, count)
        return pltpu.make_async_copy(out_hbm.at[:, cols(j)], slots.at[slot], slot_sem.at[slot])

    small = [pltpu.make_async_copy(x_hbm.at[rows_of(me), :], xrow, load_sem.at[0])]
    for i, src in enumerate((gain2_hbm, bias2_hbm, gainf_hbm, biasf_hbm)):
        small.append(pltpu.make_async_copy(src, norms.at[i], load_sem.at[i + 1]))
    for copy in small:
        copy.start()

    barrier = pltpu.get_barrier_semaphore()
    for other in (partner, cross, diag):
        pl.semaphore_signal(barrier, inc=1, device_id={"tp": other}, device_id_type=pl.DeviceIdType.MESH)
    pl.semaphore_wait(barrier, 3)

    rs = [push(near_ref.at[rows_of(1 - core), :], recv, send_sem.at[0], rs_sem.at[0], partner)]
    for copy in rs:
        copy.start()
    for n in range(n_up):
        load_up(n).start()
    for n in range(n_down):
        load_down(n).start()
    for j in range(count - first_out):
        load_out(j).start()
    for copy in small:
        copy.wait()

    def arrived(ref, sem, owner):
        pltpu.make_async_copy(ref, ref, sem.at[owner]).wait()

    arrived(recv, rs_sem, 0)
    step = 16

    def mid_rows(i, carry):
        here = pl.ds(pl.multiple_of(i * step, step), step)
        mine = pl.ds(pl.multiple_of(own_rows * me + i * step, step), step)
        summed = near_ref[pl.ds(pl.multiple_of(own_rows * core + i * step, step), step), :].astype(jnp.float32)
        for other in (recv, cross_ref, diag_ref):
            summed = summed + other[here, :].astype(jnp.float32)
        mid = (xrow[here, :].astype(jnp.float32) + summed).astype(jnp.bfloat16)
        x1[here, :] = mid
        h2[mine, :] = norm_block(mid.astype(jnp.float32), norms[0][None, :], norms[1][None, :]).astype(jnp.bfloat16)
        return carry

    lax.fori_loop(0, own_rows // step, mid_rows, 0)
    own2 = h2.at[rows_of(me), :]
    ag = [push(own2, own2, send_sem.at[3], ag_sem.at[me], cross), push(own2, own2, send_sem.at[4], ag_sem.at[me], partner)]
    for copy in ag:
        copy.start()

    def mlp_up(rows):
        def body(n, carry):
            up = jnp.dot(h2[rows, :], slots[n], preferred_element_type=jnp.float32)
            act[:, cols(n)] = jnp.square(jnp.maximum(up, 0.0)).astype(jnp.bfloat16)
            return carry

        lax.fori_loop(0, n_up, body, 0)

    def down_block(rows, n):
        part2[rows, cols(n)] = jnp.dot(act[...], slots[n_up + n], preferred_element_type=jnp.float32).astype(jnp.bfloat16)

    arrived(h2.at[rows_of(partner), :], ag_sem, partner)
    for n in range(n_up):
        load_up(n).wait()
    mlp_up(local)
    for n in range(n_down):
        load_down(n).wait()

    def down_local(n, carry):
        down_block(local, n)
        return carry

    lax.fori_loop(0, n_down, down_local, 0)
    to_partner = push(part2.at[rows_of(partner), :], recv2.at[me], send_sem.at[5], rs2_sem.at[me], partner)
    to_partner.start()
    arrived(h2.at[rows_of(cross), :], ag_sem, cross)
    relay2 = push(h2.at[rows_of(cross), :], h2.at[rows_of(cross), :], send_sem.at[6], ag_sem.at[cross], partner)
    relay2.start()
    arrived(h2.at[rows_of(diag), :], ag_sem, diag)
    mlp_up(remote)
    for j in range(count - first_out, count - n_down):
        load_out(j).start()

    def down_remote(n, carry):
        down_block(remote, n)
        for i, p in enumerate((cross, diag)):
            push(part2.at[rows_of(p), cols(n)], recv2.at[me, :, cols(n)], send_sem.at[7 + i], rs2_sem.at[me], p).start()
        return carry

    lax.fori_loop(0, n_down, down_remote, 0)
    for j in range(count - n_down, count):
        load_out(j).start()

    for p in (partner, cross, diag):
        arrived(recv2.at[p], rs2_sem, p)

    def out_rows(i, carry):
        here = pl.ds(pl.multiple_of(i * step, step), step)
        mine = pl.ds(pl.multiple_of(own_rows * me + i * step, step), step)
        summed = part2[mine, :].astype(jnp.float32)
        for p in (partner, cross, diag):
            summed = summed + recv2[p, here, :].astype(jnp.float32)
        out = (x1[here, :].astype(jnp.float32) + summed).astype(jnp.bfloat16)
        y_ref[mine, :] = out
        hf[mine, :] = norm_block(out.astype(jnp.float32), norms[2][None, :], norms[3][None, :]).astype(jnp.bfloat16)
        return carry

    lax.fori_loop(0, own_rows // step, out_rows, 0)
    ownf = hf.at[rows_of(me), :]
    owny = y_ref.at[rows_of(me), :]
    agf = [push(ownf, ownf, send_sem.at[9], agf_sem.at[me], cross), push(ownf, ownf, send_sem.at[10], agf_sem.at[me], partner)]
    agy = [push(owny, owny, send_sem.at[11], agy_sem.at[me], cross), push(owny, owny, send_sem.at[12], agy_sem.at[me], partner)]
    for copy in agf + agy:
        copy.start()

    peak[...] = jnp.full(peak.shape, -jnp.inf, jnp.float32)
    total[...] = jnp.zeros(total.shape, jnp.float32)
    lanes = peak.shape[1]

    def head_dot(rows, j, buf):
        buf[...] = jnp.dot(hf[rows, :], slots[lax.rem(j + first_out, count)], preferred_element_type=jnp.float32)

    def head_stats(rows, buf):
        old = peak[rows, :]
        new = old
        for c in range(0, wide, lanes):
            new = jnp.maximum(new, buf[:, c:c + lanes])
        acc = total[rows, :] * jnp.exp(old - new)
        for c in range(0, wide, lanes):
            acc = acc + jnp.exp(buf[:, c:c + lanes] - new)
        peak[rows, :] = new
        total[rows, :] = acc

    def head_loop(rows, size, lo, hi, before, after):
        def stage(j):
            return zst.at[lax.rem(j, 2), pl.ds(0, size), :]

        def copy_z(j):
            return pltpu.make_async_copy(stage(j), z_hbm.at[rows, cols(j)], zout_sem.at[lax.rem(j, 2)])

        before(lo)
        head_dot(rows, lo, stage(lo))
        copy_z(lo).start()
        after(lo)

        def body(j, carry):
            before(j)

            @pl.when(j >= lo + 2)
            def _():
                copy_z(j - 2).wait()

            head_stats(rows, stage(j - 1))
            head_dot(rows, j, stage(j))
            copy_z(j).start()
            after(j)
            return carry

        lax.fori_loop(lo + 1, hi, body, 0)
        head_stats(rows, stage(hi - 1))
        for j in range(hi - 2, hi):
            copy_z(j).wait()

    def nothing(j):
        pass

    def next_out(j):
        @pl.when(j + count < n_out)
        def _():
            load_out(j + count).start()

    arrived(hf.at[rows_of(partner), :], agf_sem, partner)
    head_loop(local, half, 0, RELAY, lambda j: load_out(j).wait(), nothing)
    arrived(hf.at[rows_of(cross), :], agf_sem, cross)
    relayf = push(hf.at[rows_of(cross), :], hf.at[rows_of(cross), :], send_sem.at[13], agf_sem.at[cross], partner)
    relayf.start()
    head_loop(local, half, RELAY, EARLY, lambda j: load_out(j).wait(), nothing)
    arrived(hf.at[rows_of(diag), :], agf_sem, diag)
    head_loop(remote, half, 0, EARLY, nothing, next_out)
    arrived(y_ref.at[rows_of(cross), :], agy_sem, cross)
    relayy = push(y_ref.at[rows_of(cross), :], y_ref.at[rows_of(cross), :], send_sem.at[14], agy_sem.at[cross], partner)
    relayy.start()
    head_loop(pl.ds(0, batch), batch, EARLY, n_out, lambda j: load_out(j).wait(), next_out)

    top = jnp.max(peak[...], axis=1, keepdims=True)
    bottom = jnp.sum(total[...] * jnp.exp(peak[...] - top), axis=1, keepdims=True)
    stats[me, 0] = jnp.broadcast_to(top, peak.shape).T[0:8]
    stats[me, 1] = jnp.broadcast_to(bottom, peak.shape).T[0:8]
    st = [push(stats.at[me], stats.at[me], send_sem.at[15 + i], st_sem.at[me], p) for i, p in enumerate((cross, diag, partner))]
    for copy in st:
        copy.start()
    for p in (partner, diag):
        arrived(y_ref.at[rows_of(p), :], agy_sem, p)
    for p in (partner, cross, diag):
        arrived(stats.at[p], st_sem, p)
    tops = [stats[i, 0] for i in range(4)]
    whole_top = jnp.maximum(jnp.maximum(tops[0], tops[1]), jnp.maximum(tops[2], tops[3]))
    whole = sum(stats[i, 1] * jnp.exp(tops[i] - whole_top) for i in range(4))
    lse = whole_top + jnp.log(whole)
    lse_ref[...] = jnp.broadcast_to(lse[0:1], (lanes, batch)).T

    for copy in rs + ag + [to_partner, relay2] + agf + agy + [relayf, relayy] + st:
        copy.wait_send()
    for i, p in enumerate((cross, diag)):
        push(part2.at[rows_of(p), :], recv2.at[me], send_sem.at[7 + i], rs2_sem.at[me], p).wait_send()


def subtract_kernel(hidden_ref, lse_ref, logits_hbm, y_ref, logp_hbm, buf, in_sem, out_sem):
    blocks, rows, _ = buf.shape
    ins = [pltpu.make_async_copy(logits_hbm.at[pl.ds(rows * i, rows), :], buf.at[i], in_sem.at[i]) for i in range(blocks)]
    outs = [pltpu.make_async_copy(buf.at[i], logp_hbm.at[pl.ds(rows * i, rows), :], out_sem.at[i]) for i in range(blocks)]
    for copy in ins:
        copy.start()
    y_ref[...] = hidden_ref[...]
    for i in range(blocks):
        ins[i].wait()
        buf[i] = buf[i] - lse_ref[rows * i:rows * (i + 1), 0:1]
        outs[i].start()
    for copy in outs:
        copy.wait()


def finish_layer(partials, new_hidden, ln2_gain, ln2_bias, lnf_gain, lnf_bias, w_up, w_down, w_out):
    batch, width = new_hidden.shape
    own_rows = batch // 4
    vocab = w_out.shape[1]
    vmem = pl.BlockSpec(memory_space=pltpu.VMEM)
    hbm = pl.BlockSpec(memory_space=pl.ANY)
    dma = pltpu.SemaphoreType.DMA
    bf16, f32 = jnp.bfloat16, jnp.float32
    hidden, logits, lse = pl.pallas_call(
        layer_kernel,
        out_shape=(jax.ShapeDtypeStruct((batch, width), bf16), jax.ShapeDtypeStruct((batch, vocab), f32), jax.ShapeDtypeStruct((batch, 128), f32)),
        in_specs=[vmem] * 3 + [hbm] * 8,
        out_specs=(vmem, hbm, vmem),
        scratch_shapes=[
            pltpu.VMEM((SLOTS, width, WIDE), bf16),
            pltpu.VMEM((own_rows, width), bf16),
            pltpu.VMEM((4, own_rows, width), bf16),
            pltpu.VMEM((batch, width), bf16),
            pltpu.VMEM((2 * own_rows, w_up.shape[1]), bf16),
            pltpu.VMEM((batch, width), bf16),
            pltpu.VMEM((batch, width), bf16),
            pltpu.VMEM((own_rows, width), bf16),
            pltpu.VMEM((own_rows, width), bf16),
            pltpu.VMEM((4, width), f32),
            pltpu.VMEM((2, batch, WIDE), f32),
            pltpu.VMEM((batch, 128), f32),
            pltpu.VMEM((batch, 128), f32),
            pltpu.VMEM((4, 2, 8, batch), f32),
            dma((5,)), dma((SLOTS,)), dma((2,)), dma((18,)), dma((1,)), dma((4,)), dma((4,)), dma((4,)), dma((4,)), dma((4,)),
        ],
        compiler_params=pltpu.CompilerParams(vmem_limit_bytes=VMEM_LIMIT, collective_id=0, has_side_effects=True),
        cost_estimate=pl.CostEstimate(flops=2 * batch * (w_up.size + w_down.size + w_out.size), bytes_accessed=2 * (w_up.size + w_down.size + w_out.size), transcendentals=batch * vocab),
        name="layer",
    )(*partials, new_hidden, ln2_gain, ln2_bias, lnf_gain, lnf_bias, w_up, w_down, w_out)
    blocks = 16
    return pl.pallas_call(
        subtract_kernel,
        out_shape=(jax.ShapeDtypeStruct((batch, width), bf16), jax.ShapeDtypeStruct((batch, vocab), f32)),
        in_specs=[vmem, vmem, hbm],
        out_specs=(vmem, hbm),
        scratch_shapes=[pltpu.VMEM((blocks, batch // blocks, vocab), f32), dma((blocks,)), dma((blocks,))],
        compiler_params=pltpu.CompilerParams(vmem_limit_bytes=VMEM_LIMIT),
        cost_estimate=pl.CostEstimate(flops=batch * vocab, bytes_accessed=8 * batch * vocab, transcendentals=0),
        name="subtract",
    )(hidden, lse, logits)


def solution(mesh):
    row_spec = P('bs', None)
    cache_spec = P('bs', None, 'tp', None)
    col_split = P(None, 'tp')
    row_split = P('tp', None)
    in_specs = (row_spec, cache_spec, cache_spec, P('bs'), P(), P(), col_split, col_split, col_split, row_split, P(), P(), col_split, row_split, P(), P(), col_split)
    out_specs = (P('bs', 'tp'), cache_spec, cache_spec, row_spec)

    def local_step(new_hidden, cache_k, cache_v, lengths, ln1_gain, ln1_bias, w_q, w_k, w_v, w_o, ln2_gain, ln2_bias, w_up, w_down, lnf_gain, lnf_bias, w_out):
        partials, new_cache_k, new_cache_v = attend(new_hidden, cache_k, cache_v, lengths, ln1_gain, ln1_bias, w_q, w_k, w_v, w_o)
        out_hidden, log_probs = finish_layer(partials, new_hidden, ln2_gain, ln2_bias, lnf_gain, lnf_bias, w_up, w_down, w_out)
        return log_probs, new_cache_k, new_cache_v, out_hidden

    return jax.shard_map(local_step, mesh=mesh, in_specs=in_specs, out_specs=out_specs, check_vma=False)
```

time: 147 us -> 129 us (0.88)
  other arithmetic: 11 us -> 0 us
  local copies, waits for them, and re-layouts: 11.3 us -> 0.82 us
  starting transfers between devices: 0 us -> 3.36 us
    pallas_call x1 -> x3, Pallas kernels: 34.6 us -> 51.5 us  [the longest x1 21.2 us: attend(): pl.pallas_call(far_kernel, out_shape=(shape((half // 2, width), bf16), sh...]
    pallas_call x1, Pallas kernels: 89 us -> 72.9 us  [finish_layer(): pl.pallas_call(layer_kernel, out_shape=(jax.ShapeDtypeStruct((batch, widt...]
    sub x1 -> x0, other arithmetic: 11 us -> none  [finish_layer(): return (hidden, logits - lse[:, :1])]
    broadcast_in_dim x6 -> x0, local copies, waits for them, and re-layouts: 7.84 us -> none  [the longest x1 1.31 us: attend(): ln1_bias[None, :]]
    ppermute x0 -> x2, starting transfers between devices: none -> 3.36 us  [the longest x1 3.36 us: attend(): lax.ppermute(to_cross, 'tp', [(i, (i + 2) % 4) for i in range(4)])]
  transfers between devices with their start and end apart: 0 -> 2, of which waited for: 0 -> 0; matrix products, arithmetic and copies ran while one was open for 0% -> 0% of each run, Pallas kernels for 0% -> 14%
where the time goes in v3:
time: 129 us
  Pallas kernels  124 us (96%)
  starting transfers between devices  3.36 us (3%)
    pallas_call x1, Pallas kernels, finish_layer(): pl.pallas_call(layer_kernel, out_shape=(jax.ShapeDtypeStruct((batch, widt...  72.9 us
    pallas_call x1, Pallas kernels, attend(): pl.pallas_call(far_kernel, out_shape=(shape((half // 2, width), bf16), sh...  21.2 us
    pallas_call x1, Pallas kernels, attend(): pl.pallas_call(near_kernel, out_shape=(shape((half, width), bf16), shape(...  18.2 us
    pallas_call x1, Pallas kernels, finish_layer(): pl.pallas_call(subtract_kernel, out_shape=(jax.ShapeDtypeStruct((batch, w...  12.1 us
    ppermute x1, starting transfers between devices, attend(): lax.ppermute(to_cross, 'tp', [(i, (i + 2) % 4) for i in range(4)])  3.36 us
  transfers between devices with their start and end apart: 2, of which 0 were waited for; matrix products, arithmetic and copies ran while one was open for 0% of the time, Pallas kernels for 14%

profile of v3, /device:TPU:0, one launch (start us, length us, event | category | flops | bytes accessed | tf_op | source)
XLA Modules:
  0.0 129.2 jit_solution(9434727948000500086)
XLA Ops:
  0.6 21.2 %far.1 = (bf16[64,2560]{1,0:T(8,128)(2,1)}, bf16[64,2560]{1,0:T(8,128)(2,1)}, f32[3,640,128]{2,1,0:T(8,128)}, bf16[64,8,80,256]{3,2,1,0:T(8,128)(2,1)}, bf16[64,8,80,256]{3,2,1,0:T(8,128)(2,1)}) custom-call(bf16[256,2560]{1,0:T(8,128)(2,1)} %x_hbm.1, s32[1,256]{1,0:T(1,128)} %bitcast.11, f32[2560]{0:T(1024)} %gain_ref.1, f32[2560]{0:T(1024)} %bias_ref.1, ...), custom_call_target="tpu_custom_call" | custom-call | flops 3355443200 | bytes 55050240 | tf_op jit(solution)/shard_map/far/pallas_call | solution.py:191
  21.8 3.4 %collective-permute-start = (bf16[64,2560]{1,0:T(8,128)(2,1)}, bf16[64,2560]{1,0:T(8,128)(2,1)S(1)}, u32[]{:S(2)}, u32[]{:S(2)}) collective-permute-start(bf16[64,2560]{1,0:T(8,128)(2,1)} %get-tuple-element.21), channel_id=1, source_target_pairs={{0,2},{1,3},{2,0},{3,1},{4,6},{5,7},{6,4},{7,5}} | collective-permute-start | bytes 983048 | tf_op jit(solution)/shard_map/ppermute | solution.py:211
  25.2 0.0 collective-permute-start.1
  25.2 18.2 %near.1 = (bf16[128,2560]{1,0:T(8,128)(2,1)}, bf16[64,8,80,256]{3,2,1,0:T(8,128)(2,1)}, bf16[64,8,80,256]{3,2,1,0:T(8,128)(2,1)}) custom-call(s32[1,256]{1,0:T(1,128)} %bitcast.12, f32[3,640,128]{2,1,0:T(8,128)} %get-tuple-element.17.qkv_ref, bf16[640,2560]{1,0:T(8,128)(2,1)} %wo_hbm.3, ...), custom_call_target="tpu_custom_call", output_to_operand_aliasing={{1}: (5, {}), {2}: (6, {})} | custom-call | flops 16777216000 | bytes 41943040 | tf_op jit(solution)/shard_map/near/pallas_call | solution.py:213
  43.4 0.0 collective-permute-done.cross_ref
  43.5 0.0 copy-start
  43.5 0.0 collective-permute-done.1.diag_ref
  43.5 0.0 copy-start.1
  43.5 0.7 copy-done
  44.2 0.1 copy-done.1
  44.3 72.9 %layer.1 = (bf16[256,2560]{1,0:T(8,128)(2,1)}, f32[256,12800]{1,0:T(8,128)}, f32[256,128]{1,0:T(8,128)}) custom-call(bf16[128,2560]{1,0:T(8,128)(2,1)} %get-tuple-element.20.near_ref, bf16[64,2560]{1,0:T(8,128)(2,1)} %copy-done, bf16[64,2560]{1,0:T(8,128)(2,1)} %copy-done.1, bf16[256,2560]{1,0:T(8,128)(2,1)} %x_hbm.1, f32[2560]{0:T(1024)} %gain2_hbm.1, ...), custom_call_target="tpu_custom_call" | custom-call | flops 23488102400 | bytes 91750400 | tf_op jit(solution)/shard_map/layer/pallas_call | solution.py:495
  117.2 12.1 %subtract.1 = (bf16[256,2560]{1,0:T(8,128)(2,1)}, f32[256,12800]{1,0:T(8,128)}) custom-call(bf16[256,2560]{1,0:T(8,128)(2,1)} %get-tuple-element.23.hidden_ref, f32[256,128]{1,0:T(8,128)} %get-tuple-element.24.lse_ref, f32[256,12800]{1,0:T(8,128)} %get-tuple-element.25.logits_hbm), custom_call_target="tpu_custom_call" | custom-call | flops 3276800 | bytes 26214400 | tf_op jit(solution)/shard_map/subtract/pallas_call | solution.py:522
Async XLA Ops:
  21.8 21.6 %collective-permute-start = (bf16[64,2560]{1,0:T(8,128)(2,1)}, bf16[64,2560]{1,0:T(8,128)(2,1)S(1)}, u32[]{:S(2)}, u32[]{:S(2)}) collective-permute-start(bf16[64,2560]{1,0:T(8,128)(2,1)} %get-tuple-element.21), channel_id=1, source_target_pairs={{0,2},{1,3},{2,0},{3,1},{4,6},{5,7},{6,4},{7,5}} | collective-permute-start | bytes 983048 | tf_op jit(solution)/shard_map/ppermute | solution.py:211
  25.2 18.3 %collective-permute-start.1 = (bf16[64,2560]{1,0:T(8,128)(2,1)}, bf16[64,2560]{1,0:T(8,128)(2,1)S(1)}, u32[]{:S(2)}, u32[]{:S(2)}) collective-permute-start(bf16[64,2560]{1,0:T(8,128)(2,1)} %get-tuple-element.22), channel_id=1, source_target_pairs={{0,3},{1,2},{2,1},{3,0},{4,7},{5,6},{6,5},{7,4}} | collective-permute-start | bytes 983048 | tf_op jit(solution)/shard_map/ppermute | solution.py:212
  43.5 0.7 copy-start
  43.5 0.8 copy-start.1

commit v4 on v3

--- a/solution.py
+++ b/solution.py
@@ -9,11 +9,11 @@
 EPSILON = 1e-5
 ROPE_BASE = 10000.0
 AHEAD_FAR = 6
-AHEAD_NEAR = 3
+AHEAD_NEAR = 5
 WIDE = 512
 SLOTS = 18
-EARLY = 14
-RELAY = 11
+GROUP = 5
+EARLY = 3
 VMEM_LIMIT = 66 * 1000 * 1000
 
 
@@ -91,7 +91,7 @@
         v_out(h).wait()
 
 
-def far_kernel(x_ref, len_ref, gain_ref, bias_ref, wq_hbm, wk_hbm, wv_hbm, wo_hbm, kc_hbm, vc_hbm, cross_ref, diag_ref, near_ref, ko_hbm, vo_hbm, kbuf, vbuf, wbuf, wobuf, h_ref, qkv_ref, tmp_ref, attn_ref, s_ref, far_ref, w_sem, ki_sem, vi_sem, ko_sem, vo_sem):
+def far_kernel(x_ref, len_ref, gain_ref, bias_ref, wq_hbm, wk_hbm, wv_hbm, wo_hbm, kc_hbm, vc_hbm, cross_ref, diag_ref, near_ref, own_ref, ko_hbm, vo_hbm, kbuf, vbuf, wbuf, wobuf, h_ref, qkv_ref, tmp_ref, attn_ref, s_ref, far_ref, w_sem, ki_sem, vi_sem, ko_sem, vo_sem):
     heads, cache_len, head_dim, half = kbuf.shape
     batch = x_ref.shape[0]
     half_rot = head_dim // 4
@@ -102,6 +102,8 @@
     wo_copy = pltpu.make_async_copy(wo_hbm, wobuf, w_sem.at[3])
     for copy in copies:
         copy.start()
+    own_rows = half // 2
+    own_ref[...] = x_ref[pl.ds(pl.multiple_of(own_rows * me, own_rows), own_rows), :]
     rows = 32
     gain, bias = gain_ref[...][None, :], bias_ref[...][None, :]
 
@@ -188,11 +190,11 @@
     lens = lengths[None, :]
     slabs = [pltpu.VMEM((heads, cache_len, head_dim, half), bf16)] * 2
     sems = [dma((heads,))] * 4
-    to_cross, to_diag, near, k_half, v_half = pl.pallas_call(
+    to_cross, to_diag, near, own, k_half, v_half = pl.pallas_call(
         far_kernel,
-        out_shape=(shape((half // 2, width), bf16), shape((half // 2, width), bf16), shape((3, flat, half), f32), shape(k_view.shape, bf16), shape(v_view.shape, bf16)),
+        out_shape=(shape((half // 2, width), bf16), shape((half // 2, width), bf16), shape((3, flat, half), f32), shape((half // 2, width), bf16), shape(k_view.shape, bf16), shape(v_view.shape, bf16)),
         in_specs=[vmem] * 4 + [hbm] * 6,
-        out_specs=(vmem, vmem, vmem, hbm, hbm),
+        out_specs=(vmem, vmem, vmem, vmem, hbm, hbm),
         scratch_shapes=slabs + [
             pltpu.VMEM((3, width, flat), bf16),
             pltpu.VMEM((flat, width), bf16),
@@ -226,13 +228,14 @@
         cost_estimate=pl.CostEstimate(flops=40 * batch * width * flat, bytes_accessed=4 * cache_k.size, transcendentals=0),
         name="near",
     )(lens, near, w_o, k_view, v_view, k_half, v_half)
-    return (partial, from_cross, from_diag), jnp.transpose(k_new, (3, 0, 1, 2)), jnp.transpose(v_new, (3, 0, 1, 2))
-
-
-def layer_kernel(near_ref, cross_ref, diag_ref, x_hbm, gain2_hbm, bias2_hbm, gainf_hbm, biasf_hbm, up_hbm, down_hbm, out_hbm, y_ref, z_hbm, lse_ref, slots, recv, recv2, h2, act, part2, hf, x1, xrow, norms, zst, peak, total, stats, load_sem, slot_sem, zout_sem, send_sem, rs_sem, ag_sem, rs2_sem, agf_sem, agy_sem, st_sem):
+    return (partial, from_cross, from_diag, own), jnp.transpose(k_new, (3, 0, 1, 2)), jnp.transpose(v_new, (3, 0, 1, 2))
+
+
+def layer_kernel(near_ref, cross_ref, diag_ref, xrow, gain2_ref, bias2_ref, gainf_ref, biasf_ref, up_hbm, down_hbm, out_hbm, y_hbm, z_hbm, lse_ref, y_ref, slots, recv, recv2, h2, act, act_far, part2, hf, x1, zst, peak, total, stats, load_sem, slot_sem, zout_sem, send_sem, rs_sem, ag_sem, rs2_sem, agf_sem, agy_sem, st_sem):
     batch, width = y_ref.shape
     own_rows = x1.shape[0]
     half = 2 * own_rows
+    sub = own_rows // 2
     count, _, wide = slots.shape
     n_up = up_hbm.shape[1] // wide
     n_down = down_hbm.shape[1] // wide
@@ -266,123 +269,131 @@
         slot = lax.rem(j + first_out, count)
         return pltpu.make_async_copy(out_hbm.at[:, cols(j)], slots.at[slot], slot_sem.at[slot])
 
-    small = [pltpu.make_async_copy(x_hbm.at[rows_of(me), :], xrow, load_sem.at[0])]
-    for i, src in enumerate((gain2_hbm, bias2_hbm, gainf_hbm, biasf_hbm)):
-        small.append(pltpu.make_async_copy(src, norms.at[i], load_sem.at[i + 1]))
-    for copy in small:
-        copy.start()
+    def half_of(owner, s):
+        return pl.ds(pl.multiple_of(own_rows * owner + sub * s, sub), sub)
 
     barrier = pltpu.get_barrier_semaphore()
     for other in (partner, cross, diag):
         pl.semaphore_signal(barrier, inc=1, device_id={"tp": other}, device_id_type=pl.DeviceIdType.MESH)
-    pl.semaphore_wait(barrier, 3)
-
-    rs = [push(near_ref.at[rows_of(1 - core), :], recv, send_sem.at[0], rs_sem.at[0], partner)]
-    for copy in rs:
-        copy.start()
     for n in range(n_up):
         load_up(n).start()
     for n in range(n_down):
         load_down(n).start()
-    for j in range(count - first_out):
-        load_out(j).start()
-    for copy in small:
-        copy.wait()
-
-    def arrived(ref, sem, owner):
-        pltpu.make_async_copy(ref, ref, sem.at[owner]).wait()
-
+    pl.semaphore_wait(barrier, 3)
+
+    rs = push(near_ref.at[rows_of(1 - core), :], recv, send_sem.at[0], rs_sem.at[0], partner)
+    rs.start()
+
+    def arrived(ref, sem, index):
+        pltpu.make_async_copy(ref, ref, sem.at[index]).wait()
+
+    def share(ref, sem, s, first_send):
+        rows = ref.at[half_of(me, s), :]
+        to_cross = push(rows, rows, send_sem.at[first_send], sem.at[2 * me + s], cross)
+        to_partner = push(rows, rows, send_sem.at[first_send + 1], sem.at[2 * me + s], partner)
+        to_cross.start()
+        to_partner.start()
+        return [to_cross, to_partner]
+
+    def relay(ref, sem, s, first_send):
+        rows = ref.at[half_of(cross, s), :]
+        arrived(rows, sem, 2 * cross + s)
+        copy = push(rows, rows, send_sem.at[first_send], sem.at[2 * cross + s], partner)
+        copy.start()
+        return [copy]
+
+    sent = [rs]
+    gain2, bias2 = gain2_ref[...][None, :], bias2_ref[...][None, :]
     arrived(recv, rs_sem, 0)
-    step = 16
-
-    def mid_rows(i, carry):
-        here = pl.ds(pl.multiple_of(i * step, step), step)
-        mine = pl.ds(pl.multiple_of(own_rows * me + i * step, step), step)
-        summed = near_ref[pl.ds(pl.multiple_of(own_rows * core + i * step, step), step), :].astype(jnp.float32)
+    for s in range(2):
+        here = pl.ds(sub * s, sub)
+        summed = near_ref[half_of(core, s), :].astype(jnp.float32)
         for other in (recv, cross_ref, diag_ref):
             summed = summed + other[here, :].astype(jnp.float32)
         mid = (xrow[here, :].astype(jnp.float32) + summed).astype(jnp.bfloat16)
         x1[here, :] = mid
-        h2[mine, :] = norm_block(mid.astype(jnp.float32), norms[0][None, :], norms[1][None, :]).astype(jnp.bfloat16)
-        return carry
-
-    lax.fori_loop(0, own_rows // step, mid_rows, 0)
-    own2 = h2.at[rows_of(me), :]
-    ag = [push(own2, own2, send_sem.at[3], ag_sem.at[me], cross), push(own2, own2, send_sem.at[4], ag_sem.at[me], partner)]
-    for copy in ag:
-        copy.start()
-
-    def mlp_up(rows):
-        def body(n, carry):
-            up = jnp.dot(h2[rows, :], slots[n], preferred_element_type=jnp.float32)
-            act[:, cols(n)] = jnp.square(jnp.maximum(up, 0.0)).astype(jnp.bfloat16)
-            return carry
-
-        lax.fori_loop(0, n_up, body, 0)
-
-    def down_block(rows, n):
-        part2[rows, cols(n)] = jnp.dot(act[...], slots[n_up + n], preferred_element_type=jnp.float32).astype(jnp.bfloat16)
-
-    arrived(h2.at[rows_of(partner), :], ag_sem, partner)
+        h2[half_of(me, s), :] = norm_block(mid.astype(jnp.float32), gain2, bias2).astype(jnp.bfloat16)
+        sent += share(h2, ag_sem, s, 1 + 2 * s)
+
+    def far_rows(ref, s, columns):
+        return jnp.concatenate([ref[half_of(2 * (1 - chip), s), columns], ref[half_of(2 * (1 - chip) + 1, s), columns]], axis=0)
+
+    def squared(up):
+        return jnp.square(jnp.maximum(up, 0.0)).astype(jnp.bfloat16)
+
+    def up_near():
+        for n in range(n_up):
+            act[:, wide * n:wide * (n + 1)] = squared(jnp.dot(h2[local, :], slots[n], preferred_element_type=jnp.float32))
+
+    def up_far(s):
+        for n in range(n_up):
+            act_far[:, wide * n:wide * (n + 1)] = squared(jnp.dot(far_rows(h2, s, slice(None)), slots[n], preferred_element_type=jnp.float32))
+
+    def down_near():
+        for n in range(n_down):
+            part2[local, wide * n:wide * (n + 1)] = jnp.dot(act[...], slots[n_up + n], preferred_element_type=jnp.float32).astype(jnp.bfloat16)
+
+    def send_far(p, i, s, n):
+        return push(part2.at[half_of(p, s), cols(n)], recv2.at[me, pl.ds(sub * s, sub), cols(n)], send_sem.at[5 + 2 * i + s], rs2_sem.at[2 * me + s], p)
+
+    def down_far(s):
+        for lo, hi in ((0, 2), (2, n_down)):
+            for n in range(lo, hi):
+                down = jnp.dot(act_far[...], slots[n_up + n], preferred_element_type=jnp.float32).astype(jnp.bfloat16)
+                part2[half_of(2 * (1 - chip), s), wide * n:wide * (n + 1)] = down[:sub]
+                part2[half_of(2 * (1 - chip) + 1, s), wide * n:wide * (n + 1)] = down[sub:]
+            for n in range(lo, hi):
+                for i, p in enumerate((cross, diag)):
+                    send_far(p, i, s, n).start()
+
+    for s in range(2):
+        arrived(h2.at[half_of(partner, s), :], ag_sem, 2 * partner + s)
     for n in range(n_up):
         load_up(n).wait()
-    mlp_up(local)
+    for j in range(count - first_out):
+        load_out(j).start()
+    up_near()
+    sent += relay(h2, ag_sem, 0, 9)
+    arrived(h2.at[half_of(diag, 0), :], ag_sem, 2 * diag)
+    up_far(0)
+    sent += relay(h2, ag_sem, 1, 10)
     for n in range(n_down):
         load_down(n).wait()
-
-    def down_local(n, carry):
-        down_block(local, n)
-        return carry
-
-    lax.fori_loop(0, n_down, down_local, 0)
-    to_partner = push(part2.at[rows_of(partner), :], recv2.at[me], send_sem.at[5], rs2_sem.at[me], partner)
-    to_partner.start()
-    arrived(h2.at[rows_of(cross), :], ag_sem, cross)
-    relay2 = push(h2.at[rows_of(cross), :], h2.at[rows_of(cross), :], send_sem.at[6], ag_sem.at[cross], partner)
-    relay2.start()
-    arrived(h2.at[rows_of(diag), :], ag_sem, diag)
-    mlp_up(remote)
+    down_far(0)
+    arrived(h2.at[half_of(diag, 1), :], ag_sem, 2 * diag + 1)
+    up_far(1)
     for j in range(count - first_out, count - n_down):
         load_out(j).start()
-
-    def down_remote(n, carry):
-        down_block(remote, n)
-        for i, p in enumerate((cross, diag)):
-            push(part2.at[rows_of(p), cols(n)], recv2.at[me, :, cols(n)], send_sem.at[7 + i], rs2_sem.at[me], p).start()
-        return carry
-
-    lax.fori_loop(0, n_down, down_remote, 0)
+    down_far(1)
+    down_near()
     for j in range(count - n_down, count):
         load_out(j).start()
-
-    for p in (partner, cross, diag):
-        arrived(recv2.at[p], rs2_sem, p)
-
-    def out_rows(i, carry):
-        here = pl.ds(pl.multiple_of(i * step, step), step)
-        mine = pl.ds(pl.multiple_of(own_rows * me + i * step, step), step)
-        summed = part2[mine, :].astype(jnp.float32)
+    for s in range(2):
+        copy = push(part2.at[half_of(partner, s), :], recv2.at[me, pl.ds(sub * s, sub), :], send_sem.at[11 + s], rs2_sem.at[2 * me + s], partner)
+        copy.start()
+        sent.append(copy)
+
+    gainf, biasf = gainf_ref[...][None, :], biasf_ref[...][None, :]
+    for s in range(2):
+        here = pl.ds(sub * s, sub)
+        for p in (partner, cross, diag):
+            arrived(recv2.at[p, here, :], rs2_sem, 2 * p + s)
+        summed = part2[half_of(me, s), :].astype(jnp.float32)
         for p in (partner, cross, diag):
             summed = summed + recv2[p, here, :].astype(jnp.float32)
         out = (x1[here, :].astype(jnp.float32) + summed).astype(jnp.bfloat16)
-        y_ref[mine, :] = out
-        hf[mine, :] = norm_block(out.astype(jnp.float32), norms[2][None, :], norms[3][None, :]).astype(jnp.bfloat16)
-        return carry
-
-    lax.fori_loop(0, own_rows // step, out_rows, 0)
-    ownf = hf.at[rows_of(me), :]
+        y_ref[half_of(me, s), :] = out
+        hf[half_of(me, s), :] = norm_block(out.astype(jnp.float32), gainf, biasf).astype(jnp.bfloat16)
+        sent += share(hf, agf_sem, s, 13 + 2 * s)
     owny = y_ref.at[rows_of(me), :]
-    agf = [push(ownf, ownf, send_sem.at[9], agf_sem.at[me], cross), push(ownf, ownf, send_sem.at[10], agf_sem.at[me], partner)]
-    agy = [push(owny, owny, send_sem.at[11], agy_sem.at[me], cross), push(owny, owny, send_sem.at[12], agy_sem.at[me], partner)]
-    for copy in agf + agy:
+    for i, p in enumerate((cross, partner)):
+        copy = push(owny, owny, send_sem.at[17 + i], agy_sem.at[me], p)
         copy.start()
+        sent.append(copy)
 
     peak[...] = jnp.full(peak.shape, -jnp.inf, jnp.float32)
     total[...] = jnp.zeros(total.shape, jnp.float32)
     lanes = peak.shape[1]
-
-    def head_dot(rows, j, buf):
-        buf[...] = jnp.dot(hf[rows, :], slots[lax.rem(j + first_out, count)], preferred_element_type=jnp.float32)
 
     def head_stats(rows, buf):
         old = peak[rows, :]
@@ -396,65 +407,78 @@
         total[rows, :] = acc
 
     def head_loop(rows, size, lo, hi, before, after):
-        def stage(j):
-            return zst.at[lax.rem(j, 2), pl.ds(0, size), :]
-
-        def copy_z(j):
-            return pltpu.make_async_copy(stage(j), z_hbm.at[rows, cols(j)], zout_sem.at[lax.rem(j, 2)])
-
-        before(lo)
-        head_dot(rows, lo, stage(lo))
-        copy_z(lo).start()
-        after(lo)
-
-        def body(j, carry):
-            before(j)
-
-            @pl.when(j >= lo + 2)
+        def stage(g, i):
+            return zst.at[lax.rem(g, 2), i, pl.ds(0, size), :]
+
+        def copy_z(g, i):
+            return pltpu.make_async_copy(stage(g, i), z_hbm.at[rows, cols(GROUP * g + i)], zout_sem.at[lax.rem(g, 2), i])
+
+        def body(g, carry):
+            for i in range(GROUP):
+                before(GROUP * g + i)
+
+            @pl.when(g >= lo + 2)
             def _():
-                copy_z(j - 2).wait()
-
-            head_stats(rows, stage(j - 1))
-            head_dot(rows, j, stage(j))
-            copy_z(j).start()
-            after(j)
+                for i in range(GROUP):
+                    copy_z(g - 2, i).wait()
+
+            for i in range(GROUP):
+                stage(g, i)[...] = jnp.dot(hf[rows, :], slots[lax.rem(GROUP * g + i + first_out, count)], preferred_element_type=jnp.float32)
+                head_stats(rows, stage(g, i))
+            for i in range(GROUP):
+                copy_z(g, i).start()
+            after(g)
             return carry
 
-        lax.fori_loop(lo + 1, hi, body, 0)
-        head_stats(rows, stage(hi - 1))
-        for j in range(hi - 2, hi):
-            copy_z(j).wait()
+        lax.fori_loop(lo, hi, body, 0)
+        for g in range(max(lo, hi - 2), hi):
+            for i in range(GROUP):
+                copy_z(g, i).wait()
 
     def nothing(j):
         pass
 
-    def next_out(j):
-        @pl.when(j + count < n_out)
-        def _():
-            load_out(j + count).start()
-
-    arrived(hf.at[rows_of(partner), :], agf_sem, partner)
-    head_loop(local, half, 0, RELAY, lambda j: load_out(j).wait(), nothing)
-    arrived(hf.at[rows_of(cross), :], agf_sem, cross)
-    relayf = push(hf.at[rows_of(cross), :], hf.at[rows_of(cross), :], send_sem.at[13], agf_sem.at[cross], partner)
-    relayf.start()
-    head_loop(local, half, RELAY, EARLY, lambda j: load_out(j).wait(), nothing)
-    arrived(hf.at[rows_of(diag), :], agf_sem, diag)
+    def next_out(g):
+        for i in range(GROUP):
+            @pl.when(GROUP * g + i + count < n_out)
+            def _():
+                load_out(GROUP * g + i + count).start()
+
+    def ready(j):
+        load_out(j).wait()
+
+    for s in range(2):
+        arrived(hf.at[half_of(partner, s), :], agf_sem, 2 * partner + s)
+    relays = [push(hf.at[half_of(cross, s), :], hf.at[half_of(cross, s), :], send_sem.at[19 + s], agf_sem.at[2 * cross + s], partner) for s in range(2)]
+
+    def pass_on(g):
+        for s in range(2):
+            @pl.when(g == s)
+            def _():
+                arrived(hf.at[half_of(cross, s), :], agf_sem, 2 * cross + s)
+                relays[s].start()
+
+    head_loop(local, half, 0, EARLY, ready, pass_on)
+    sent += relays
+    for s in range(2):
+        arrived(hf.at[half_of(diag, s), :], agf_sem, 2 * diag + s)
     head_loop(remote, half, 0, EARLY, nothing, next_out)
     arrived(y_ref.at[rows_of(cross), :], agy_sem, cross)
-    relayy = push(y_ref.at[rows_of(cross), :], y_ref.at[rows_of(cross), :], send_sem.at[14], agy_sem.at[cross], partner)
+    relayy = push(y_ref.at[rows_of(cross), :], y_ref.at[rows_of(cross), :], send_sem.at[21], agy_sem.at[cross], partner)
     relayy.start()
-    head_loop(pl.ds(0, batch), batch, EARLY, n_out, lambda j: load_out(j).wait(), next_out)
-
+    head_loop(pl.ds(0, batch), batch, EARLY, n_out // GROUP, ready, next_out)
+
+    for p in (partner, diag):
+        arrived(y_ref.at[rows_of(p), :], agy_sem, p)
+    y_copy = pltpu.make_async_copy(y_ref, y_hbm, load_sem.at[0])
+    y_copy.start()
     top = jnp.max(peak[...], axis=1, keepdims=True)
     bottom = jnp.sum(total[...] * jnp.exp(peak[...] - top), axis=1, keepdims=True)
     stats[me, 0] = jnp.broadcast_to(top, peak.shape).T[0:8]
     stats[me, 1] = jnp.broadcast_to(bottom, peak.shape).T[0:8]
-    st = [push(stats.at[me], stats.at[me], send_sem.at[15 + i], st_sem.at[me], p) for i, p in enumerate((cross, diag, partner))]
+    st = [push(stats.at[me], stats.at[me], send_sem.at[22 + i], st_sem.at[me], p) for i, p in enumerate((cross, diag, partner))]
     for copy in st:
         copy.start()
-    for p in (partner, diag):
-        arrived(y_ref.at[rows_of(p), :], agy_sem, p)
     for p in (partner, cross, diag):
         arrived(stats.at[p], st_sem, p)
     tops = [stats[i, 0] for i in range(4)]
@@ -463,24 +487,31 @@
     lse = whole_top + jnp.log(whole)
     lse_ref[...] = jnp.broadcast_to(lse[0:1], (lanes, batch)).T
 
-    for copy in rs + ag + [to_partner, relay2] + agf + agy + [relayf, relayy] + st:
+    y_copy.wait()
+    for copy in sent + [relayy] + st:
         copy.wait_send()
     for i, p in enumerate((cross, diag)):
-        push(part2.at[rows_of(p), :], recv2.at[me], send_sem.at[7 + i], rs2_sem.at[me], p).wait_send()
-
-
-def subtract_kernel(hidden_ref, lse_ref, logits_hbm, y_ref, logp_hbm, buf, in_sem, out_sem):
+        for s in range(2):
+            whole_half = part2.at[half_of(p, s), :]
+            push(whole_half, recv2.at[me, pl.ds(sub * s, sub), :], send_sem.at[5 + 2 * i + s], rs2_sem.at[2 * me + s], p).wait_send()
+
+
+def subtract_kernel(lse_ref, hidden_hbm, logits_hbm, y_hbm, logp_hbm, y_buf, buf, y_sem, in_sem, out_sem):
     blocks, rows, _ = buf.shape
     ins = [pltpu.make_async_copy(logits_hbm.at[pl.ds(rows * i, rows), :], buf.at[i], in_sem.at[i]) for i in range(blocks)]
     outs = [pltpu.make_async_copy(buf.at[i], logp_hbm.at[pl.ds(rows * i, rows), :], out_sem.at[i]) for i in range(blocks)]
+    y_in = pltpu.make_async_copy(hidden_hbm, y_buf, y_sem.at[0])
+    y_out = pltpu.make_async_copy(y_buf, y_hbm, y_sem.at[1])
     for copy in ins:
         copy.start()
-    y_ref[...] = hidden_ref[...]
+    y_in.start()
     for i in range(blocks):
         ins[i].wait()
         buf[i] = buf[i] - lse_ref[rows * i:rows * (i + 1), 0:1]
         outs[i].start()
-    for copy in outs:
+    y_in.wait()
+    y_out.start()
+    for copy in outs + [y_out]:
         copy.wait()
 
 
@@ -495,40 +526,40 @@
     hidden, logits, lse = pl.pallas_call(
         layer_kernel,
         out_shape=(jax.ShapeDtypeStruct((batch, width), bf16), jax.ShapeDtypeStruct((batch, vocab), f32), jax.ShapeDtypeStruct((batch, 128), f32)),
-        in_specs=[vmem] * 3 + [hbm] * 8,
-        out_specs=(vmem, hbm, vmem),
+        in_specs=[vmem] * 8 + [hbm] * 3,
+        out_specs=(hbm, hbm, vmem),
         scratch_shapes=[
+            pltpu.VMEM((batch, width), bf16),
             pltpu.VMEM((SLOTS, width, WIDE), bf16),
             pltpu.VMEM((own_rows, width), bf16),
             pltpu.VMEM((4, own_rows, width), bf16),
             pltpu.VMEM((batch, width), bf16),
             pltpu.VMEM((2 * own_rows, w_up.shape[1]), bf16),
+            pltpu.VMEM((own_rows, w_up.shape[1]), bf16),
             pltpu.VMEM((batch, width), bf16),
             pltpu.VMEM((batch, width), bf16),
             pltpu.VMEM((own_rows, width), bf16),
-            pltpu.VMEM((own_rows, width), bf16),
-            pltpu.VMEM((4, width), f32),
-            pltpu.VMEM((2, batch, WIDE), f32),
+            pltpu.VMEM((2, GROUP, batch, WIDE), f32),
             pltpu.VMEM((batch, 128), f32),
             pltpu.VMEM((batch, 128), f32),
             pltpu.VMEM((4, 2, 8, batch), f32),
-            dma((5,)), dma((SLOTS,)), dma((2,)), dma((18,)), dma((1,)), dma((4,)), dma((4,)), dma((4,)), dma((4,)), dma((4,)),
+            dma((1,)), dma((SLOTS,)), dma((2, GROUP)), dma((25,)), dma((1,)), dma((8,)), dma((8,)), dma((8,)), dma((4,)), dma((4,)),
         ],
         compiler_params=pltpu.CompilerParams(vmem_limit_bytes=VMEM_LIMIT, collective_id=0, has_side_effects=True),
         cost_estimate=pl.CostEstimate(flops=2 * batch * (w_up.size + w_down.size + w_out.size), bytes_accessed=2 * (w_up.size + w_down.size + w_out.size), transcendentals=batch * vocab),
         name="layer",
-    )(*partials, new_hidden, ln2_gain, ln2_bias, lnf_gain, lnf_bias, w_up, w_down, w_out)
+    )(*partials, ln2_gain, ln2_bias, lnf_gain, lnf_bias, w_up, w_down, w_out)
     blocks = 16
     return pl.pallas_call(
         subtract_kernel,
         out_shape=(jax.ShapeDtypeStruct((batch, width), bf16), jax.ShapeDtypeStruct((batch, vocab), f32)),
-        in_specs=[vmem, vmem, hbm],
-        out_specs=(vmem, hbm),
-        scratch_shapes=[pltpu.VMEM((blocks, batch // blocks, vocab), f32), dma((blocks,)), dma((blocks,))],
+        in_specs=[vmem, hbm, hbm],
+        out_specs=(hbm, hbm),
+        scratch_shapes=[pltpu.VMEM((batch, width), bf16), pltpu.VMEM((blocks, batch // blocks, vocab), f32), dma((2,)), dma((blocks,)), dma((blocks,))],
         compiler_params=pltpu.CompilerParams(vmem_limit_bytes=VMEM_LIMIT),
         cost_estimate=pl.CostEstimate(flops=batch * vocab, bytes_accessed=8 * batch * vocab, transcendentals=0),
         name="subtract",
-    )(hidden, lse, logits)
+    )(lse, hidden, logits)
 
 
 def solution(mesh):

time: 129 us -> 117 us (0.907)
  Pallas kernels: 124 us -> 112 us
    pallas_call x1, Pallas kernels: 72.9 us -> 61.5 us  [finish_layer(): pl.pallas_call(layer_kernel, out_shape=(jax.ShapeDtypeStruct((batch, widt...]
  transfers between devices with their start and end apart: 2 -> 2, of which waited for: 0 -> 0; matrix products, arithmetic and copies ran while one was open for 0% -> 0% of each run, Pallas kernels for 14% -> 15%
where the time goes in v4:
time: 117 us
  Pallas kernels  112 us (96%)
  starting transfers between devices  3.35 us (3%)
    pallas_call x1, Pallas kernels, finish_layer(): pl.pallas_call(layer_kernel, out_shape=(jax.ShapeDtypeStruct((batch, widt...  61.5 us
    pallas_call x1, Pallas kernels, attend(): pl.pallas_call(far_kernel, out_shape=(shape((half // 2, width), bf16), sh...  21.3 us
    pallas_call x1, Pallas kernels, attend(): pl.pallas_call(near_kernel, out_shape=(shape((half, width), bf16), shape(...  17.7 us
    pallas_call x1, Pallas kernels, finish_layer(): pl.pallas_call(subtract_kernel, out_shape=(jax.ShapeDtypeStruct((batch, w...  11.4 us
    ppermute x1, starting transfers between devices, attend(): lax.ppermute(to_cross, 'tp', [(i, (i + 2) % 4) for i in range(4)])  3.35 us
  transfers between devices with their start and end apart: 2, of which 0 were waited for; matrix products, arithmetic and copies ran while one was open for 0% of the time, Pallas kernels for 15%

profile of v4, /device:TPU:0, one launch (start us, length us, event | category | flops | bytes accessed | tf_op | source)
XLA Modules:
  0.0 116.9 jit_solution(10905602004678776260)
XLA Ops:
  0.6 21.3 %far.1 = (bf16[64,2560]{1,0:T(8,128)(2,1)}, bf16[64,2560]{1,0:T(8,128)(2,1)}, f32[3,640,128]{2,1,0:T(8,128)}, bf16[64,2560]{1,0:T(8,128)(2,1)}, bf16[64,8,80,256...) custom-call(bf16[256,2560]{1,0:T(8,128)(2,1)} %x_ref.1, s32[1,256]{1,0:T(1,128)} %bitcast.11, f32[2560]{0:T(1024)} %gain_ref.1, ...), custom_call_target="tpu_custom_call" | custom-call | flops 3355443200 | bytes 55050240 | tf_op jit(solution)/shard_map/far/pallas_call | solution.py:193
  21.9 3.4 %collective-permute-start = (bf16[64,2560]{1,0:T(8,128)(2,1)}, bf16[64,2560]{1,0:T(8,128)(2,1)S(1)}, u32[]{:S(2)}, u32[]{:S(2)}) collective-permute-start(bf16[64,2560]{1,0:T(8,128)(2,1)} %get-tuple-element.22), channel_id=1, source_target_pairs={{0,2},{1,3},{2,0},{3,1},{4,6},{5,7},{6,4},{7,5}} | collective-permute-start | bytes 983048 | tf_op jit(solution)/shard_map/ppermute | solution.py:213
  25.2 0.0 collective-permute-start.1
  25.2 17.7 %near.1 = (bf16[128,2560]{1,0:T(8,128)(2,1)}, bf16[64,8,80,256]{3,2,1,0:T(8,128)(2,1)}, bf16[64,8,80,256]{3,2,1,0:T(8,128)(2,1)}) custom-call(s32[1,256]{1,0:T(1,128)} %bitcast.12, f32[3,640,128]{2,1,0:T(8,128)} %get-tuple-element.18.qkv_ref, bf16[640,2560]{1,0:T(8,128)(2,1)} %wo_hbm.3, ...), custom_call_target="tpu_custom_call", output_to_operand_aliasing={{1}: (5, {}), {2}: (6, {})} | custom-call | flops 16777216000 | bytes 41943040 | tf_op jit(solution)/shard_map/near/pallas_call | solution.py:215
  43.0 0.0 collective-permute-done.cross_ref
  43.0 0.0 copy-start
  43.0 0.0 collective-permute-done.1.diag_ref
  43.0 0.0 copy-start.1
  43.0 0.7 copy-done
  43.7 0.1 copy-done.1
  43.8 61.5 %layer.1 = (bf16[256,2560]{1,0:T(8,128)(2,1)}, f32[256,12800]{1,0:T(8,128)}, f32[256,128]{1,0:T(8,128)}) custom-call(bf16[128,2560]{1,0:T(8,128)(2,1)} %get-tuple-element.21.near_ref, bf16[64,2560]{1,0:T(8,128)(2,1)} %copy-done, bf16[64,2560]{1,0:T(8,128)(2,1)} %copy-done.1, bf16[64,2560]{1,0:T(8,128)(2,1)} %get-tuple-element.24.xrow, f32[2560]{0:T(1024)} %gain2_ref.1, ...), custom_call_target="tpu_custom_call" | custom-call | flops 23488102400 | bytes 91750400 | tf_op jit(solution)/shard_map/layer/pallas_call | solution.py:526
  105.3 11.4 %subtract.1 = (bf16[256,2560]{1,0:T(8,128)(2,1)}, f32[256,12800]{1,0:T(8,128)}) custom-call(f32[256,128]{1,0:T(8,128)} %get-tuple-element.25.lse_ref, bf16[256,2560]{1,0:T(8,128)(2,1)} %get-tuple-element.26.hidden_hbm, f32[256,12800]{1,0:T(8,128)} %get-tuple-element.27.logits_hbm), custom_call_target="tpu_custom_call" | custom-call | flops 3276800 | bytes 26214400 | tf_op jit(solution)/shard_map/subtract/pallas_call | solution.py:553
Async XLA Ops:
  21.9 21.1 %collective-permute-start = (bf16[64,2560]{1,0:T(8,128)(2,1)}, bf16[64,2560]{1,0:T(8,128)(2,1)S(1)}, u32[]{:S(2)}, u32[]{:S(2)}) collective-permute-start(bf16[64,2560]{1,0:T(8,128)(2,1)} %get-tuple-element.22), channel_id=1, source_target_pairs={{0,2},{1,3},{2,0},{3,1},{4,6},{5,7},{6,4},{7,5}} | collective-permute-start | bytes 983048 | tf_op jit(solution)/shard_map/ppermute | solution.py:213
  25.2 17.7 %collective-permute-start.1 = (bf16[64,2560]{1,0:T(8,128)(2,1)}, bf16[64,2560]{1,0:T(8,128)(2,1)S(1)}, u32[]{:S(2)}, u32[]{:S(2)}) collective-permute-start(bf16[64,2560]{1,0:T(8,128)(2,1)} %get-tuple-element.23), channel_id=1, source_target_pairs={{0,3},{1,2},{2,1},{3,0},{4,7},{5,6},{6,5},{7,4}} | collective-permute-start | bytes 983048 | tf_op jit(solution)/shard_map/ppermute | solution.py:214
  43.0 0.7 copy-start
  43.0 0.8 copy-start.1

commit v5 on v4

--- a/solution.py
+++ b/solution.py
@@ -8,11 +8,12 @@
 
 EPSILON = 1e-5
 ROPE_BASE = 10000.0
-AHEAD_FAR = 6
+AHEAD_FAR = 5
 AHEAD_NEAR = 5
 WIDE = 512
 SLOTS = 18
 GROUP = 5
+WINDOW = 4
 EARLY = 3
 VMEM_LIMIT = 66 * 1000 * 1000
 
@@ -337,7 +338,7 @@
         return push(part2.at[half_of(p, s), cols(n)], recv2.at[me, pl.ds(sub * s, sub), cols(n)], send_sem.at[5 + 2 * i + s], rs2_sem.at[2 * me + s], p)
 
     def down_far(s):
-        for lo, hi in ((0, 2), (2, n_down)):
+        for lo, hi in ((0, 1), (1, 3), (3, n_down)):
             for n in range(lo, hi):
                 down = jnp.dot(act_far[...], slots[n_up + n], preferred_element_type=jnp.float32).astype(jnp.bfloat16)
                 part2[half_of(2 * (1 - chip), s), wide * n:wide * (n + 1)] = down[:sub]
@@ -406,34 +407,46 @@
         peak[rows, :] = new
         total[rows, :] = acc
 
-    def head_loop(rows, size, lo, hi, before, after):
-        def stage(g, i):
-            return zst.at[lax.rem(g, 2), i, pl.ds(0, size), :]
-
-        def copy_z(g, i):
-            return pltpu.make_async_copy(stage(g, i), z_hbm.at[rows, cols(GROUP * g + i)], zout_sem.at[lax.rem(g, 2), i])
+    everyone = pl.ds(0, batch)
+    turns = [(local, half, g) for g in range(EARLY)] + [(remote, half, g) for g in range(EARLY)] + [(everyone, batch, g) for g in range(EARLY, n_out // GROUP)]
+
+    def copy_z(rows, size, g, parity, i):
+        return pltpu.make_async_copy(zst.at[parity, i, pl.ds(0, size), :], z_hbm.at[rows, cols(GROUP * g + i)], zout_sem.at[parity, i])
+
+    def finish_turn(turn):
+        rows, size, g = turns[turn]
+        for i in range(GROUP):
+            copy_z(rows, size, g, turn % 2, i).wait()
+
+    def head_loop(first, last, before, after):
+        rows, size, lo = turns[first]
+        hi = turns[last][2] + 1
 
         def body(g, carry):
+            parity = lax.rem(g - lo + first, 2)
             for i in range(GROUP):
                 before(GROUP * g + i)
+            for ago in range(2):
+                if first + ago >= 2:
+                    @pl.when(g == lo + ago)
+                    def _():
+                        finish_turn(first + ago - 2)
 
             @pl.when(g >= lo + 2)
             def _():
                 for i in range(GROUP):
-                    copy_z(g - 2, i).wait()
+                    copy_z(rows, size, g - 2, parity, i).wait()
 
             for i in range(GROUP):
-                stage(g, i)[...] = jnp.dot(hf[rows, :], slots[lax.rem(GROUP * g + i + first_out, count)], preferred_element_type=jnp.float32)
-                head_stats(rows, stage(g, i))
+                stage = zst.at[parity, i, pl.ds(0, size), :]
+                stage[...] = jnp.dot(hf[rows, :], slots[lax.rem(GROUP * g + i + first_out, count)], preferred_element_type=jnp.float32)
+                head_stats(rows, stage)
             for i in range(GROUP):
-                copy_z(g, i).start()
+                copy_z(rows, size, g, parity, i).start()
             after(g)
             return carry
 
         lax.fori_loop(lo, hi, body, 0)
-        for g in range(max(lo, hi - 2), hi):
-            for i in range(GROUP):
-                copy_z(g, i).wait()
 
     def nothing(j):
         pass
@@ -458,15 +471,15 @@
                 arrived(hf.at[half_of(cross, s), :], agf_sem, 2 * cross + s)
                 relays[s].start()
 
-    head_loop(local, half, 0, EARLY, ready, pass_on)
+    head_loop(0, EARLY - 1, ready, pass_on)
     sent += relays
     for s in range(2):
         arrived(hf.at[half_of(diag, s), :], agf_sem, 2 * diag + s)
-    head_loop(remote, half, 0, EARLY, nothing, next_out)
+    head_loop(EARLY, 2 * EARLY - 1, nothing, next_out)
     arrived(y_ref.at[rows_of(cross), :], agy_sem, cross)
     relayy = push(y_ref.at[rows_of(cross), :], y_ref.at[rows_of(cross), :], send_sem.at[21], agy_sem.at[cross], partner)
     relayy.start()
-    head_loop(pl.ds(0, batch), batch, EARLY, n_out // GROUP, ready, next_out)
+    head_loop(2 * EARLY, len(turns) - 1, ready, next_out)
 
     for p in (partner, diag):
         arrived(y_ref.at[rows_of(p), :], agy_sem, p)
@@ -487,6 +500,8 @@
     lse = whole_top + jnp.log(whole)
     lse_ref[...] = jnp.broadcast_to(lse[0:1], (lanes, batch)).T
 
+    for turn in (len(turns) - 2, len(turns) - 1):
+        finish_turn(turn)
     y_copy.wait()
     for copy in sent + [relayy] + st:
         copy.wait_send()
@@ -502,10 +517,12 @@
     outs = [pltpu.make_async_copy(buf.at[i], logp_hbm.at[pl.ds(rows * i, rows), :], out_sem.at[i]) for i in range(blocks)]
     y_in = pltpu.make_async_copy(hidden_hbm, y_buf, y_sem.at[0])
     y_out = pltpu.make_async_copy(y_buf, y_hbm, y_sem.at[1])
-    for copy in ins:
+    for copy in ins[:WINDOW]:
         copy.start()
     y_in.start()
     for i in range(blocks):
+        if i + WINDOW < blocks:
+            ins[i + WINDOW].start()
         ins[i].wait()
         buf[i] = buf[i] - lse_ref[rows * i:rows * (i + 1), 0:1]
         outs[i].start()
@@ -549,7 +566,7 @@
         cost_estimate=pl.CostEstimate(flops=2 * batch * (w_up.size + w_down.size + w_out.size), bytes_accessed=2 * (w_up.size + w_down.size + w_out.size), transcendentals=batch * vocab),
         name="layer",
     )(*partials, ln2_gain, ln2_bias, lnf_gain, lnf_bias, w_up, w_down, w_out)
-    blocks = 16
+    blocks = 8
     return pl.pallas_call(
         subtract_kernel,
         out_shape=(jax.ShapeDtypeStruct((batch, width), bf16), jax.ShapeDtypeStruct((batch, vocab), f32)),

time: 117 us -> 113 us (0.966)
  Pallas kernels: 112 us -> 108 us
    pallas_call x1, Pallas kernels: 61.5 us -> 57.9 us  [finish_layer(): pl.pallas_call(layer_kernel, out_shape=(jax.ShapeDtypeStruct((batch, widt...]
  transfers between devices with their start and end apart: 2 -> 2, of which waited for: 0 -> 0; matrix products, arithmetic and copies ran while one was open for 0% -> 0% of each run, Pallas kernels for 15% -> 16%
where the time goes in v5:
time: 113 us
  Pallas kernels  108 us (96%)
  starting transfers between devices  3.36 us (3%)
    pallas_call x1, Pallas kernels, finish_layer(): pl.pallas_call(layer_kernel, out_shape=(jax.ShapeDtypeStruct((batch, widt...  57.9 us
    pallas_call x1, Pallas kernels, attend(): pl.pallas_call(far_kernel, out_shape=(shape((half // 2, width), bf16), sh...  21.1 us
    pallas_call x1, Pallas kernels, attend(): pl.pallas_call(near_kernel, out_shape=(shape((half, width), bf16), shape(...  17.7 us
    pallas_call x1, Pallas kernels, finish_layer(): pl.pallas_call(subtract_kernel, out_shape=(jax.ShapeDtypeStruct((batch, w...  10.9 us
    ppermute x1, starting transfers between devices, attend(): lax.ppermute(to_cross, 'tp', [(i, (i + 2) % 4) for i in range(4)])  3.36 us
  transfers between devices with their start and end apart: 2, of which 0 were waited for; matrix products, arithmetic and copies ran while one was open for 0% of the time, Pallas kernels for 16%

profile of v5, /device:TPU:0, one launch (start us, length us, event | category | flops | bytes accessed | tf_op | source)
XLA Modules:
  0.0 112.7 jit_solution(8534132250747240718)
XLA Ops:
  0.6 21.1 %far.1 = (bf16[64,2560]{1,0:T(8,128)(2,1)}, bf16[64,2560]{1,0:T(8,128)(2,1)}, f32[3,640,128]{2,1,0:T(8,128)}, bf16[64,2560]{1,0:T(8,128)(2,1)}, bf16[64,8,80,256...) custom-call(bf16[256,2560]{1,0:T(8,128)(2,1)} %x_ref.1, s32[1,256]{1,0:T(1,128)} %bitcast.11, f32[2560]{0:T(1024)} %gain_ref.1, ...), custom_call_target="tpu_custom_call" | custom-call | flops 3355443200 | bytes 55050240 | tf_op jit(solution)/shard_map/far/pallas_call | solution.py:194
  21.7 3.4 %collective-permute-start = (bf16[64,2560]{1,0:T(8,128)(2,1)}, bf16[64,2560]{1,0:T(8,128)(2,1)S(1)}, u32[]{:S(2)}, u32[]{:S(2)}) collective-permute-start(bf16[64,2560]{1,0:T(8,128)(2,1)} %get-tuple-element.22), channel_id=1, source_target_pairs={{0,2},{1,3},{2,0},{3,1},{4,6},{5,7},{6,4},{7,5}} | collective-permute-start | bytes 983048 | tf_op jit(solution)/shard_map/ppermute | solution.py:214
  25.1 0.0 collective-permute-start.1
  25.1 17.7 %near.1 = (bf16[128,2560]{1,0:T(8,128)(2,1)}, bf16[64,8,80,256]{3,2,1,0:T(8,128)(2,1)}, bf16[64,8,80,256]{3,2,1,0:T(8,128)(2,1)}) custom-call(s32[1,256]{1,0:T(1,128)} %bitcast.12, f32[3,640,128]{2,1,0:T(8,128)} %get-tuple-element.18.qkv_ref, bf16[640,2560]{1,0:T(8,128)(2,1)} %wo_hbm.3, ...), custom_call_target="tpu_custom_call", output_to_operand_aliasing={{1}: (5, {}), {2}: (6, {})} | custom-call | flops 16777216000 | bytes 41943040 | tf_op jit(solution)/shard_map/near/pallas_call | solution.py:216
  42.8 0.0 collective-permute-done.cross_ref
  42.8 0.0 copy-start
  42.8 0.0 collective-permute-done.1.diag_ref
  42.8 0.0 copy-start.1
  42.9 0.7 copy-done
  43.6 0.1 copy-done.1
  43.7 57.9 %layer.1 = (bf16[256,2560]{1,0:T(8,128)(2,1)}, f32[256,12800]{1,0:T(8,128)}, f32[256,128]{1,0:T(8,128)}) custom-call(bf16[128,2560]{1,0:T(8,128)(2,1)} %get-tuple-element.21.near_ref, bf16[64,2560]{1,0:T(8,128)(2,1)} %copy-done, bf16[64,2560]{1,0:T(8,128)(2,1)} %copy-done.1, bf16[64,2560]{1,0:T(8,128)(2,1)} %get-tuple-element.24.xrow, f32[2560]{0:T(1024)} %gain2_ref.1, ...), custom_call_target="tpu_custom_call" | custom-call | flops 23488102400 | bytes 91750400 | tf_op jit(solution)/shard_map/layer/pallas_call | solution.py:543
  101.6 10.9 %subtract.1 = (bf16[256,2560]{1,0:T(8,128)(2,1)}, f32[256,12800]{1,0:T(8,128)}) custom-call(f32[256,128]{1,0:T(8,128)} %get-tuple-element.25.lse_ref, bf16[256,2560]{1,0:T(8,128)(2,1)} %get-tuple-element.26.hidden_hbm, f32[256,12800]{1,0:T(8,128)} %get-tuple-element.27.logits_hbm), custom_call_target="tpu_custom_call" | custom-call | flops 3276800 | bytes 26214400 | tf_op jit(solution)/shard_map/subtract/pallas_call | solution.py:570
Async XLA Ops:
  21.7 21.1 %collective-permute-start = (bf16[64,2560]{1,0:T(8,128)(2,1)}, bf16[64,2560]{1,0:T(8,128)(2,1)S(1)}, u32[]{:S(2)}, u32[]{:S(2)}) collective-permute-start(bf16[64,2560]{1,0:T(8,128)(2,1)} %get-tuple-element.22), channel_id=1, source_target_pairs={{0,2},{1,3},{2,0},{3,1},{4,6},{5,7},{6,4},{7,5}} | collective-permute-start | bytes 983048 | tf_op jit(solution)/shard_map/ppermute | solution.py:214
  25.1 17.7 %collective-permute-start.1 = (bf16[64,2560]{1,0:T(8,128)(2,1)}, bf16[64,2560]{1,0:T(8,128)(2,1)S(1)}, u32[]{:S(2)}, u32[]{:S(2)}) collective-permute-start(bf16[64,2560]{1,0:T(8,128)(2,1)} %get-tuple-element.23), channel_id=1, source_target_pairs={{0,3},{1,2},{2,1},{3,0},{4,7},{5,6},{6,5},{7,4}} | collective-permute-start | bytes 983048 | tf_op jit(solution)/shard_map/ppermute | solution.py:215
  42.8 0.7 copy-start
  42.8 0.8 copy-start.1
